TPU v7x, 16 devices: a whole 2x2x2 slice. The times are simulated.
16 devices in a mesh: dp: 4 (over z, y), tp: 4 (over x, core).
Axes of the slice: x: 2, y: 2, z: 2, core: 2. Of those that a mesh axis runs over, the one named last changes fastest.
Arguments:
- tokens: bfloat16 [4, 6144, 3072], P('dp', 'tp'), parts along dimension 0
- cond_vec: float32 [4, 3072], P('dp'), parts along dimension 0
- txt_len: int32 [4], P('dp'), parts along dimension 0
- grid_hw: int32 [4, 2], P('dp'), parts along dimension 0
- w_mod: bfloat16 [3072, 9216], replicated
- b_mod: float32 [9216], replicated
- w_qkv: bfloat16 [3072, 3, 3072], P(None, None, 'tp')
- b_qkv: float32 [3, 3072], P(None, 'tp')
- q_gain: float32 [128], replicated
- k_gain: float32 [128], replicated
- w_mlp_in: bfloat16 [3072, 12288], P(None, 'tp')
- b_mlp_in: float32 [12288], P('tp')
- w_out_attn: bfloat16 [3072, 3072], P('tp')
- w_out_mlp: bfloat16 [12288, 3072], P('tp')
- b_out: float32 [3072], replicated
Outputs:
- output: bfloat16 [4, 6144, 3072], P('dp', 'tp'), parts along dimension 0
There are 4 independent parts. A program takes and returns all parts, laid end to end along the dimension named above; an argument that names none is the same for every part.
All inputs are finite; a program needn't handle non-finite values.
Results may differ from a plain program's by a relative error of at most 0.00356712.
Values are sent between devices in bfloat16 or wider.
A program may use at most 1 GiB of HBM per device.

v0:
```python
import jax
import jax.numpy as jnp
from jax import lax
from jax.sharding import PartitionSpec as P

HEAD = 128
TXT = 256
QBLOCK = 256
EPS = 1e-6
THETA = 256.0


def modulation(cond_vec, w_mod, b_mod):
    d_model = w_mod.shape[0]
    mod_all = jnp.dot(jax.nn.silu(cond_vec).astype(jnp.bfloat16), w_mod, preferred_element_type=jnp.float32) + b_mod
    return mod_all[:, :d_model], mod_all[:, d_model:2 * d_model], mod_all[:, 2 * d_model:]


def modulated_norm(tokens, shift, scale):
    tok_f32 = tokens.astype(jnp.float32)
    centered = tok_f32 - jnp.mean(tok_f32, axis=-1, keepdims=True)
    variance = jnp.mean(centered * centered, axis=-1, keepdims=True)
    normed = centered * lax.rsqrt(variance + EPS)
    return (normed * (1.0 + scale[:, None, :]) + shift[:, None, :]).astype(jnp.bfloat16)


def rope_table(grid_hw, seq_len):
    tok_idx = jnp.arange(seq_len, dtype=jnp.int32)[None, :]
    grid_h = grid_hw[:, 0:1]
    grid_w = grid_hw[:, 1:2]
    t_pos = tok_idx // (grid_h * grid_w)
    h_pos = (tok_idx // grid_w) % grid_h
    w_pos = tok_idx % grid_w
    pair_idx = jnp.arange(HEAD // 2, dtype=jnp.int32)
    axis_sel = (pair_idx >= 8).astype(jnp.int32) + (pair_idx >= 36).astype(jnp.int32)
    within = pair_idx - jnp.where(axis_sel == 0, 0, jnp.where(axis_sel == 1, 8, 36))
    axis_dim = jnp.where(axis_sel == 0, 16.0, 56.0)
    inv_freq = jnp.power(THETA, -2.0 * within.astype(jnp.float32) / axis_dim)
    pos_sel = jnp.where(axis_sel == 0, t_pos[..., None], jnp.where(axis_sel == 1, h_pos[..., None], w_pos[..., None]))
    angles = pos_sel.astype(jnp.float32) * inv_freq
    angles = jnp.where((tok_idx < seq_len - TXT)[..., None], angles, 0.0)
    return jnp.cos(angles), jnp.sin(angles)


def apply_rope(heads_f32, cos_t, sin_t):
    full_shape = heads_f32.shape
    pairs = heads_f32.reshape(full_shape[:-1] + (full_shape[-1] // 2, 2))
    real_part = pairs[..., 0]
    imag_part = pairs[..., 1]
    cos_b = cos_t[:, :, None, :]
    sin_b = sin_t[:, :, None, :]
    rotated = jnp.stack([real_part * cos_b - imag_part * sin_b, real_part * sin_b + imag_part * cos_b], axis=-1)
    return rotated.reshape(full_shape)


def head_rms(heads_f32, gain):
    mean_sq = jnp.mean(heads_f32 * heads_f32, axis=-1, keepdims=True)
    return heads_f32 * lax.rsqrt(mean_sq + EPS) * gain


def attention(q_heads, k_heads, v_heads, tok_valid):
    batch, seq_len, n_heads, head_dim = q_heads.shape
    qk_scale = head_dim ** -0.5
    def one_block(block_id):
        q_blk = lax.dynamic_slice_in_dim(q_heads, block_id * QBLOCK, QBLOCK, axis=1)
        q_valid = lax.dynamic_slice_in_dim(tok_valid, block_id * QBLOCK, QBLOCK, axis=1)
        same_seg = q_valid[:, :, None] == tok_valid[:, None, :]
        scores = jnp.einsum('bqhd,bkhd->bhqk', q_blk, k_heads, preferred_element_type=jnp.float32) * qk_scale
        scores = jnp.where(same_seg[:, None, :, :], scores, -1e30)
        probs = jax.nn.softmax(scores, axis=-1).astype(jnp.bfloat16)
        return jnp.einsum('bhqk,bkhd->bqhd', probs, v_heads, preferred_element_type=jnp.float32).astype(jnp.bfloat16)
    blocks = lax.map(one_block, jnp.arange(seq_len // QBLOCK))
    return jnp.moveaxis(blocks, 0, 1).reshape(batch, seq_len, n_heads, head_dim)


def branch_partial(y_mod, txt_len, grid_hw, w_qkv, b_qkv, q_gain, k_gain, w_mlp_in, b_mlp_in, w_out_attn, w_out_mlp):
    batch = y_mod.shape[0]
    seq_len = y_mod.shape[1]
    d_local = w_qkv.shape[2]
    head_shape = (batch, seq_len, d_local // HEAD, HEAD)
    qkv_f32 = jnp.einsum('bnd,dce->bnce', y_mod, w_qkv, preferred_element_type=jnp.float32) + b_qkv
    cos_t, sin_t = rope_table(grid_hw, seq_len)
    q_heads = apply_rope(head_rms(qkv_f32[:, :, 0].reshape(head_shape), q_gain), cos_t, sin_t).astype(jnp.bfloat16)
    k_heads = apply_rope(head_rms(qkv_f32[:, :, 1].reshape(head_shape), k_gain), cos_t, sin_t).astype(jnp.bfloat16)
    v_heads = qkv_f32[:, :, 2].reshape(head_shape).astype(jnp.bfloat16)
    tok_valid = jnp.arange(seq_len)[None, :] < (seq_len - TXT + txt_len)[:, None]
    attended = attention(q_heads, k_heads, v_heads, tok_valid).reshape(batch, seq_len, d_local)
    mlp_pre = jnp.einsum('bnd,df->bnf', y_mod, w_mlp_in, preferred_element_type=jnp.float32) + b_mlp_in
    mlp_act = jax.nn.gelu(mlp_pre, approximate=True).astype(jnp.bfloat16)
    attn_part = jnp.einsum('bnc,ce->bne', attended, w_out_attn, preferred_element_type=jnp.float32)
    mlp_part = jnp.einsum('bnf,fe->bne', mlp_act, w_out_mlp, preferred_element_type=jnp.float32)
    return attn_part + mlp_part


def solution(mesh):
    def local_step(tokens, cond_vec, txt_len, grid_hw, w_mod, b_mod, w_qkv, b_qkv, q_gain, k_gain, w_mlp_in, b_mlp_in, w_out_attn, w_out_mlp, b_out):
        shift, scale, gate = modulation(cond_vec, w_mod, b_mod)
        y_local = modulated_norm(tokens, shift, scale)
        y_full = lax.all_gather(y_local, 'tp', axis=1, tiled=True)
        part_sum = branch_partial(y_full, txt_len, grid_hw, w_qkv, b_qkv, q_gain, k_gain, w_mlp_in, b_mlp_in, w_out_attn, w_out_mlp)
        own_sum = lax.psum_scatter(part_sum, 'tp', scatter_dimension=1, tiled=True)
        result = tokens.astype(jnp.float32) + gate[:, None, :] * (own_sum + b_out)
        return result.astype(jnp.bfloat16)
    in_specs = (P('dp', 'tp', None), P('dp', None), P('dp'), P('dp', None), P(None, None), P(None), P(None, None, 'tp'), P(None, 'tp'), P(None), P(None), P(None, 'tp'), P('tp'), P('tp', None), P('tp', None), P(None))
    return jax.shard_map(local_step, mesh=mesh, in_specs=in_specs, out_specs=P('dp', 'tp', None), check_vma=False)
```

profile of v0, /device:TPU:0, one launch (start us, length us, event | category | flops | bytes accessed | tf_op | source)
XLA Modules:
  0.0 3408.4 jit_solution(14753124547592714535)
XLA Ops:
  68.6 204.5 %all-gather.2.cloned.1.call-done = bf16[1,6144,3072]{2,1,0:T(8,128)(2,1)} async-done(((bf16[1,1536,3072]{2,1,0:T(8,128)(2,1)}), bf16[1,6144,3072]{2,1,0:T(8,128)(2,1)}) %all-gather.2.cloned.1.call-update) | async-done | bytes 37748752 | tf_op jit(solution)/shard_map/all_gather | solution.py:99
  273.0 98.0 %add_bitcast_fusion.1 = f32[1,6144,3,768]{1,3,2,0:T(8,128)} fusion(f32[3,768]{1,0:T(4,128)S(1)} %copy-done.10, bf16[3072,3,768]{2,0,1:T(8,128)(2,1)} %param.27, bf16[1,6144,3072]{2,1,0:T(8,128)(2,1)} %all-gather.2.cloned.1.call-done), kind=kOutput, calls=%fused_computation.32 | convolution fusion | flops 86987243520 | bytes 108536832 | tf_op jit(solution)/shard_map/bnd,dce->bnce/dot_general | solution.py:81
  506.0 53.7 %subtract_convert_fusion = (bf16[1,6144,6,64,1]{1,4,3,2,0:T(2,128)(2,1)}, bf16[1,6144,6,64,1]{1,4,3,2,0:T(2,128)(2,1)}, bf16[1,6144,6,64,1]{1,4,3,2,0:T(2,128)(2,1)}, bf16[1,6144,6,64,1]{1,4,3,2,0:T(2,128)(2,1)}) fusion(f32[1,6144,6,64,2]{1,4,3,2,0:T(2,128)} %get-tuple-element.94, f32[6144,64]{0,1:T(8,128)S(1)} %copy-done.2, f32[6144,64]{0,1:T(8,128)S(1)} %copy-done.1, ...), kind=kLoop, calls=%fused_computation.52 | loop fusion | flops 37748736 | bytes 59768832 | tf_op jit(solution)/shard_map/convert.1
  656.9 1897.6 %while.10 = (s32[]{:T(128)}, bf16[24,1,256,6,128]{4,2,3,1,0:T(8,128)(2,1)}, s32[24]{0:T(128)S(1)}, pred[1,6144]{1,0:T(4,128)(4,1)S(1)}, bf16[1,6144,6,128]{1,3,2...) while((s32[]{:T(128)}, ...), condition=%wide.region_7.10_spmd, body=%wide.region_4.9_spmd.sunk | while | flops 4909111296 | bytes 173833664 | solution.py:72
  676.9 41.4 %fusion.76 = (f32[6,256]{1,0:T(8,128)S(1)}, f32[6,256,6144]{2,1,0:T(8,128)}) fusion(f32[6,256,6144]{2,1,0:T(8,128)} %fusion.75, pred[256,6144]{1,0:T(8,128)(4,1)S(1)} %broadcast_compare_fusion.4), kind=kOutput, calls=%fused_computation.92.clone.1 | output fusion | flops 56629248 | bytes 77076480 | tf_op jit(solution)/shard_map/while/body/eval_jaxpr/sub | solution.py:70
  755.9 41.4 %fusion.76 = (f32[6,256]{1,0:T(8,128)S(1)}, f32[6,256,6144]{2,1,0:T(8,128)}) fusion(f32[6,256,6144]{2,1,0:T(8,128)} %fusion.75, pred[256,6144]{1,0:T(8,128)(4,1)S(1)} %broadcast_compare_fusion.4), kind=kOutput, calls=%fused_computation.92.clone.1 | output fusion | flops 56629248 | bytes 77076480 | tf_op jit(solution)/shard_map/while/body/eval_jaxpr/sub | solution.py:70
  835.0 41.4 %fusion.76 = (f32[6,256]{1,0:T(8,128)S(1)}, f32[6,256,6144]{2,1,0:T(8,128)}) fusion(f32[6,256,6144]{2,1,0:T(8,128)} %fusion.75, pred[256,6144]{1,0:T(8,128)(4,1)S(1)} %broadcast_compare_fusion.4), kind=kOutput, calls=%fused_computation.92.clone.1 | output fusion | flops 56629248 | bytes 77076480 | tf_op jit(solution)/shard_map/while/body/eval_jaxpr/sub | solution.py:70
  914.0 41.4 %fusion.76 = (f32[6,256]{1,0:T(8,128)S(1)}, f32[6,256,6144]{2,1,0:T(8,128)}) fusion(f32[6,256,6144]{2,1,0:T(8,128)} %fusion.75, pred[256,6144]{1,0:T(8,128)(4,1)S(1)} %broadcast_compare_fusion.4), kind=kOutput, calls=%fused_computation.92.clone.1 | output fusion | flops 56629248 | bytes 77076480 | tf_op jit(solution)/shard_map/while/body/eval_jaxpr/sub | solution.py:70
  993.1 41.4 %fusion.76 = (f32[6,256]{1,0:T(8,128)S(1)}, f32[6,256,6144]{2,1,0:T(8,128)}) fusion(f32[6,256,6144]{2,1,0:T(8,128)} %fusion.75, pred[256,6144]{1,0:T(8,128)(4,1)S(1)} %broadcast_compare_fusion.4), kind=kOutput, calls=%fused_computation.92.clone.1 | output fusion | flops 56629248 | bytes 77076480 | tf_op jit(solution)/shard_map/while/body/eval_jaxpr/sub | solution.py:70
  1072.1 41.4 %fusion.76 = (f32[6,256]{1,0:T(8,128)S(1)}, f32[6,256,6144]{2,1,0:T(8,128)}) fusion(f32[6,256,6144]{2,1,0:T(8,128)} %fusion.75, pred[256,6144]{1,0:T(8,128)(4,1)S(1)} %broadcast_compare_fusion.4), kind=kOutput, calls=%fused_computation.92.clone.1 | output fusion | flops 56629248 | bytes 77076480 | tf_op jit(solution)/shard_map/while/body/eval_jaxpr/sub | solution.py:70
  1704.5 41.4 %fusion.76 = (f32[6,256]{1,0:T(8,128)S(1)}, f32[6,256,6144]{2,1,0:T(8,128)}) fusion(f32[6,256,6144]{2,1,0:T(8,128)} %fusion.75, pred[256,6144]{1,0:T(8,128)(4,1)S(1)} %broadcast_compare_fusion.4), kind=kOutput, calls=%fused_computation.92.clone.1 | output fusion | flops 56629248 | bytes 77076480 | tf_op jit(solution)/shard_map/while/body/eval_jaxpr/sub | solution.py:70
  1783.6 41.4 %fusion.76 = (f32[6,256]{1,0:T(8,128)S(1)}, f32[6,256,6144]{2,1,0:T(8,128)}) fusion(f32[6,256,6144]{2,1,0:T(8,128)} %fusion.75, pred[256,6144]{1,0:T(8,128)(4,1)S(1)} %broadcast_compare_fusion.4), kind=kOutput, calls=%fused_computation.92.clone.1 | output fusion | flops 56629248 | bytes 77076480 | tf_op jit(solution)/shard_map/while/body/eval_jaxpr/sub | solution.py:70
  1862.6 41.4 %fusion.76 = (f32[6,256]{1,0:T(8,128)S(1)}, f32[6,256,6144]{2,1,0:T(8,128)}) fusion(f32[6,256,6144]{2,1,0:T(8,128)} %fusion.75, pred[256,6144]{1,0:T(8,128)(4,1)S(1)} %broadcast_compare_fusion.4), kind=kOutput, calls=%fused_computation.92.clone.1 | output fusion | flops 56629248 | bytes 77076480 | tf_op jit(solution)/shard_map/while/body/eval_jaxpr/sub | solution.py:70
  1941.7 41.4 %fusion.76 = (f32[6,256]{1,0:T(8,128)S(1)}, f32[6,256,6144]{2,1,0:T(8,128)}) fusion(f32[6,256,6144]{2,1,0:T(8,128)} %fusion.75, pred[256,6144]{1,0:T(8,128)(4,1)S(1)} %broadcast_compare_fusion.4), kind=kOutput, calls=%fused_computation.92.clone.1 | output fusion | flops 56629248 | bytes 77076480 | tf_op jit(solution)/shard_map/while/body/eval_jaxpr/sub | solution.py:70
  2020.7 41.4 %fusion.76 = (f32[6,256]{1,0:T(8,128)S(1)}, f32[6,256,6144]{2,1,0:T(8,128)}) fusion(f32[6,256,6144]{2,1,0:T(8,128)} %fusion.75, pred[256,6144]{1,0:T(8,128)(4,1)S(1)} %broadcast_compare_fusion.4), kind=kOutput, calls=%fused_computation.92.clone.1 | output fusion | flops 56629248 | bytes 77076480 | tf_op jit(solution)/shard_map/while/body/eval_jaxpr/sub | solution.py:70
  2099.8 41.4 %fusion.76 = (f32[6,256]{1,0:T(8,128)S(1)}, f32[6,256,6144]{2,1,0:T(8,128)}) fusion(f32[6,256,6144]{2,1,0:T(8,128)} %fusion.75, pred[256,6144]{1,0:T(8,128)(4,1)S(1)} %broadcast_compare_fusion.4), kind=kOutput, calls=%fused_computation.92.clone.1 | output fusion | flops 56629248 | bytes 77076480 | tf_op jit(solution)/shard_map/while/body/eval_jaxpr/sub | solution.py:70
  2178.8 41.4 %fusion.76 = (f32[6,256]{1,0:T(8,128)S(1)}, f32[6,256,6144]{2,1,0:T(8,128)}) fusion(f32[6,256,6144]{2,1,0:T(8,128)} %fusion.75, pred[256,6144]{1,0:T(8,128)(4,1)S(1)} %broadcast_compare_fusion.4), kind=kOutput, calls=%fused_computation.92.clone.1 | output fusion | flops 56629248 | bytes 77076480 | tf_op jit(solution)/shard_map/while/body/eval_jaxpr/sub | solution.py:70
  2257.9 41.4 %fusion.76 = (f32[6,256]{1,0:T(8,128)S(1)}, f32[6,256,6144]{2,1,0:T(8,128)}) fusion(f32[6,256,6144]{2,1,0:T(8,128)} %fusion.75, pred[256,6144]{1,0:T(8,128)(4,1)S(1)} %broadcast_compare_fusion.4), kind=kOutput, calls=%fused_computation.92.clone.1 | output fusion | flops 56629248 | bytes 77076480 | tf_op jit(solution)/shard_map/while/body/eval_jaxpr/sub | solution.py:70
  2336.9 41.4 %fusion.76 = (f32[6,256]{1,0:T(8,128)S(1)}, f32[6,256,6144]{2,1,0:T(8,128)}) fusion(f32[6,256,6144]{2,1,0:T(8,128)} %fusion.75, pred[256,6144]{1,0:T(8,128)(4,1)S(1)} %broadcast_compare_fusion.4), kind=kOutput, calls=%fused_computation.92.clone.1 | output fusion | flops 56629248 | bytes 77076480 | tf_op jit(solution)/shard_map/while/body/eval_jaxpr/sub | solution.py:70
  2416.0 41.4 %fusion.76 = (f32[6,256]{1,0:T(8,128)S(1)}, f32[6,256,6144]{2,1,0:T(8,128)}) fusion(f32[6,256,6144]{2,1,0:T(8,128)} %fusion.75, pred[256,6144]{1,0:T(8,128)(4,1)S(1)} %broadcast_compare_fusion.4), kind=kOutput, calls=%fused_computation.92.clone.1 | output fusion | flops 56629248 | bytes 77076480 | tf_op jit(solution)/shard_map/while/body/eval_jaxpr/sub | solution.py:70
  2495.0 41.4 %fusion.76 = (f32[6,256]{1,0:T(8,128)S(1)}, f32[6,256,6144]{2,1,0:T(8,128)}) fusion(f32[6,256,6144]{2,1,0:T(8,128)} %fusion.75, pred[256,6144]{1,0:T(8,128)(4,1)S(1)} %broadcast_compare_fusion.4), kind=kOutput, calls=%fused_computation.92.clone.1 | output fusion | flops 56629248 | bytes 77076480 | tf_op jit(solution)/shard_map/while/body/eval_jaxpr/sub | solution.py:70
  2618.4 146.9 %fusion.30 = bf16[6144,3072]{1,0:T(8,128)(2,1)} fusion(bf16[3072,3072]{1,0:T(8,128)(2,1)} %param.31, bf16[1,6144,3072]{2,1,0:T(8,128)(2,1)} %all-gather.2.cloned.1.call-done, f32[3072]{0:T(1024)S(1)} %copy-done.11), kind=kOutput, calls=%fused_computation.30 | convolution fusion | flops 116152860672 | bytes 94384128 | tf_op jit(solution)/shard_map/bnd,df->bnf/dot_general | solution.py:88
  2765.3 128.9 %add_bitcast_fusion = f32[1,6144,3072]{2,1,0:T(8,128)} fusion(f32[6144,3072]{1,0:T(8,128)} %fusion.58, bf16[6144,3072]{1,0:T(8,128)(2,1)} %fusion.30, bf16[3072,3072]{1,0:T(8,128)(2,1)} %param.34), kind=kOutput, calls=%fused_computation.31 | convolution fusion | flops 115982991360 | bytes 207618048 | tf_op jit(solution)/shard_map/bnf,fe->bne/dot_general | solution.py:91
  2894.2 492.9 %reduce-scatter.2.cloned.1.call-done = f32[1,1536,3072]{2,1,0:T(8,128)} async-done(((f32[1,6144,3072]{2,1,0:T(8,128)}), f32[1,1536,3072]{2,1,0:T(8,128)}) %reduce-scatter.2.cloned.1.call-update) | async-done | bytes 18874384 | tf_op jit(solution)/shard_map/reduce_scatter | solution.py:101
  (219 shorter events, 1546.4 us)
Async XLA Ops:
  6.5 20.3 copy-start.5
  6.5 266.5 %all-gather.2.cloned.1.call-start = ((), (), s32[]{:S(2)}) async-start(), calls=%async_computation.1 | async-start | bytes 47185920 | tf_op jit(solution)/shard_map/all_gather | solution.py:99
  6.5 21.0 copy-start
  28.8 16.1 copy-start.7
  28.8 21.3 copy-start.8
  28.9 22.0 copy-start.9
  28.9 244.2 %copy-start.10 = (f32[3,768]{1,0:T(4,128)S(1)}, f32[3,768]{1,0:T(4,128)}, u32[]{:S(2)}) copy-start(f32[3,768]{1,0:T(4,128)} %param.28) | copy-start | bytes 27652
  44.3 3342.8 %reduce-scatter.2.cloned.1.call-start = ((), (), s32[]{:S(2)}) async-start(), calls=%async_computation.2 | async-start | bytes 94371840 | tf_op jit(solution)/shard_map/reduce_scatter | solution.py:101
  475.8 30.2 copy-start.1
  475.8 30.2 copy-start.2
  630.5 26.4 copy-start.3
  2578.7 39.7 %copy-start.11 = (f32[3072]{0:T(1024)S(1)}, f32[3072]{0:T(1024)}, u32[]{:S(2)}) copy-start(f32[3072]{0:T(1024)} %param.32) | copy-start | bytes 36868
  2894.2 492.9 %copy-start.4 = (f32[1,3072]{1,0:T(1,128)S(1)}, f32[1,3072]{1,0:T(1,128)}, u32[]{:S(2)}) copy-start(f32[1,3072]{1,0:T(1,128)} %get-tuple-element.87) | copy-start | bytes 36868
  2894.2 492.9 %copy-start.6 = (f32[3072]{0:T(1024)S(1)}, f32[3072]{0:T(1024)}, u32[]{:S(2)}) copy-start(f32[3072]{0:T(1024)} %param.35) | copy-start | bytes 36868
Sparse Core Ops, SparseCore 0:
  44.4 228.5 all-gather.1
  2894.3 492.6 reduce-scatter.1
where the time goes:
time: 3410 us
  matrix products  1280 us (38%)
  other arithmetic  1250 us (37%)
  waiting for transfers between devices  697 us (20%)
  local copies, waits for them, and re-layouts  147 us (4%)
    sub x24, other arithmetic, one_block(): probs = jax.nn.softmax(scores, axis=-1).astype(jnp.bfloat16)  994 us
    reduce_scatter x1, waiting for transfers between devices, local_step(): own_sum = lax.psum_scatter(part_sum, 'tp', scatter_dimension=1, tiled=True)  493 us
    dot_general x24, matrix products, one_block(): jnp.einsum('bhqk,bkhd->bqhd', probs, v_heads, preferred_element_type=jnp....  434 us
    dot_general x24, matrix products, one_block(): jnp.einsum('bqhd,bkhd->bhqk', q_blk, k_heads, preferred_element_type=jnp....  415 us
    all_gather x1, waiting for transfers between devices, local_step(): y_full = lax.all_gather(y_local, 'tp', axis=1, tiled=True)  204 us
    dot_general x1, matrix products, branch_partial(): jnp.einsum('bnd,df->bnf', y_mod, w_mlp_in, preferred_element_type=jnp.flo...  147 us
    dot_general x1, matrix products, branch_partial(): jnp.einsum('bnf,fe->bne', mlp_act, w_out_mlp, preferred_element_type=jnp....  129 us
    dot_general x1, matrix products, branch_partial(): jnp.einsum('bnd,dce->bnce', y_mod, w_qkv, preferred_element_type=jnp.floa...  98 us
  transfers between devices with their start and end apart: 2, of which 2 were waited for; matrix products, arithmetic and copies ran while one was open for 1% of the time, Pallas kernels for 0%

commit v1 on v0

v1 whole, which is shorter than its diff:
```python
import functools
import jax
import jax.numpy as jnp
from jax import lax
from jax.experimental import pallas as pl
from jax.experimental.pallas import tpu as pltpu
from jax.sharding import PartitionSpec as P


SEQ = 6144
D = 3072
HD = 128
TXT = 256
VID = SEQ - TXT
EPS = 1e-6
THETA = 256.0
SHARD = 1536
CHIP = 2 * SHARD
DQ = 768
LOG2E = 1.4426950408889634
BF = jnp.bfloat16
F32 = jnp.float32
NT = (((1,), (1,)), ((), ()))
X_PAIRS = [(0, 2), (1, 3), (2, 0), (3, 1)]
C_PAIRS = [(0, 1), (1, 0), (2, 3), (3, 2)]


def params(mib=60, **kw):
    return pltpu.CompilerParams(vmem_limit_bytes=mib * 2 ** 20, **kw)


def cost(flops, nbytes):
    return pl.CostEstimate(flops=int(flops), bytes_accessed=int(nbytes), transcendentals=0)


def norm_kernel(x_ref, scale_ref, shift_ref, y_ref):
    x = x_ref[...].astype(F32)
    c = x - jnp.mean(x, axis=-1, keepdims=True)
    var = jnp.mean(c * c, axis=-1, keepdims=True)
    y_ref[...] = (c * lax.rsqrt(var + EPS) * scale_ref[...] + shift_ref[...]).astype(BF)


def norm(x, scale1, shift):
    bm = 256
    n = x.shape[0]
    row = pl.BlockSpec((1, D), lambda i: (0, 0))
    blk = pl.BlockSpec((bm, D), lambda i: (i, 0))
    return pl.pallas_call(norm_kernel, grid=(n // bm,), in_specs=[blk, row, row], out_specs=blk,
                          out_shape=jax.ShapeDtypeStruct((n, D), BF), compiler_params=params(),
                          cost_estimate=cost(n * D * 8, n * D * 4), name="norm")(x, scale1, shift)


QBM = 512
SUB = 256


def qkv_kernel(half, off_ref, y0_ref, y1_ref, w_ref, b_ref, qg_ref, kg_ref, cos_ref, sin_ref, *refs):
    q_ref, k_ref, vt_ref, left0, left1 = refs[-5:]
    n = pl.program_id(1)
    tiles = [(i, s) for i in range(QBM // SUB) for s in range(DQ // SUB)]
    pairs = [tiles[a:a + 2] for a in range(0, len(tiles), 2)]

    def proj(y_ref, t):
        return jnp.dot(y_ref[pl.ds(t[0] * SUB, SUB), :], w_ref[0, :, pl.ds(t[1] * SUB, SUB)], preferred_element_type=F32)

    def rope(r, t, gain_ref, row, out_ref):
        at = pl.ds(t[0] * SUB, SUB)
        even = lax.broadcasted_iota(jnp.int32, (SUB, HD), 1) % 2 == 0
        for h in range(SUB // HD):
            lo = t[1] * SUB + h * HD
            x = r[:, h * HD:(h + 1) * HD] + b_ref[row:row + 1, lo:lo + HD]
            ms = jnp.mean(x * x, axis=-1, keepdims=True)
            x = x * lax.rsqrt(ms + EPS) * gain_ref[...]
            partner = jnp.where(even, pltpu.roll(x, HD - 1, 1), pltpu.roll(x, 1, 1))
            out_ref[at, lo:lo + HD] = (x * cos_ref[at, :] + partner * sin_ref[at, :]).astype(BF)

    def put(r, t):
        lo = t[1] * SUB
        vt_ref[pl.ds(lo, SUB), pl.ds(t[0] * SUB, SUB)] = (r + b_ref[2:3, lo:lo + SUB]).T.astype(BF)

    def q_epi(r, t):
        rope(r, t, qg_ref, 0, q_ref)

    def k_epi(r, t):
        rope(r, t, kg_ref, 1, k_ref)

    def run(y_ref, epi, before, keep):
        held = []
        for p, pair in enumerate(pairs):
            last = keep and p == len(pairs) - 1
            now = [(proj(y_ref, t), t) for t in pair]
            if last:
                left0[...] = now[0][0]
                left1[...] = now[1][0]
            if p == 0 and before is not None:
                before(left0[...], pairs[-1][0])
                before(left1[...], pairs[-1][1])
            for r, t in held:
                epi(r, t)
            held = [] if last else now
        for r, t in held:
            epi(r, t)

    def step(y_ref):
        @pl.when(n == 0)
        def _():
            run(y_ref, q_epi, None, True)

        @pl.when(n == 1)
        def _():
            run(y_ref, k_epi, q_epi, True)

        @pl.when(n == 2)
        def _():
            run(y_ref, put, k_epi, False)

    if half is None:
        step(y0_ref)
    else:
        @pl.when(pl.program_id(0) < half)
        def _():
            step(y0_ref)

        @pl.when(pl.program_id(0) >= half)
        def _():
            step(y1_ref)


def qkv(off, ys, w3, b, qg, kg, cos, sin, prev=None):
    m0 = ys[0].shape[0] // QBM
    half = m0 if len(ys) == 2 else None
    m = m0 * len(ys)
    at = lambda i, o: jnp.where(i < m0, o[0] + i, o[1] + i - m0)
    in_specs = [pl.BlockSpec((QBM, D), lambda i, n, o: (jnp.minimum(i, m0 - 1), 0)),
                pl.BlockSpec((QBM, D), (lambda i, n, o: (jnp.maximum(i - m0, 0), 0)) if half else (lambda i, n, o: (0, 0))),
                pl.BlockSpec((1, D, DQ), lambda i, n, o: (n, 0, 0)),
                pl.BlockSpec((3, DQ), lambda i, n, o: (0, 0)),
                pl.BlockSpec((1, HD), lambda i, n, o: (0, 0)),
                pl.BlockSpec((1, HD), lambda i, n, o: (0, 0)),
                pl.BlockSpec((QBM, HD), lambda i, n, o: (at(i, o), 0)),
                pl.BlockSpec((QBM, HD), lambda i, n, o: (at(i, o), 0))]
    args = [off, ys[0], ys[-1], w3, b, qg, kg, cos, sin]
    if half is None:
        in_specs[1] = pl.BlockSpec(memory_space=pl.ANY)
    alias = {}
    if prev is not None:
        in_specs += [pl.BlockSpec(memory_space=pl.ANY)] * 3
        args += list(prev)
        alias = {9: 0, 10: 1, 11: 2}
    return pl.pallas_call(
        functools.partial(qkv_kernel, half),
        grid_spec=pltpu.PrefetchScalarGridSpec(
            num_scalar_prefetch=1, grid=(m, 3), in_specs=in_specs,
            out_specs=[pl.BlockSpec((QBM, DQ), lambda i, n, o: (at(i, o), 0)),
                       pl.BlockSpec((QBM, DQ), lambda i, n, o: (at(i, o), 0)),
                       pl.BlockSpec((DQ, QBM), lambda i, n, o: (0, at(i, o)))],
            scratch_shapes=[pltpu.VMEM((SUB, SUB), F32)] * 2),
        out_shape=[jax.ShapeDtypeStruct((SEQ, DQ), BF), jax.ShapeDtypeStruct((SEQ, DQ), BF),
                   jax.ShapeDtypeStruct((DQ, SEQ), BF)],
        input_output_aliases=alias, compiler_params=params(),
        cost_estimate=cost(2 * m * QBM * D * 3 * DQ, m * QBM * D * 2 + 3 * D * DQ * 2), name="qkv")(*args)


BQ = 1536
BK = 512


def attn_kernel(sc_ref, q_ref, k_ref, vt_ref, o_ref, flag_ref):
    i = pl.program_id(1)
    txt_len = sc_ref[1]

    @pl.when(i == 0)
    def _():
        vmax = jnp.max(jnp.abs(vt_ref[...].astype(F32)))
        flag_ref[0] = jnp.logical_and(vmax <= 4096.0, sc_ref[2] == 1).astype(jnp.int32)

    bq = q_ref.shape[0]
    nk = SEQ // BK
    last = BK - TXT
    first_row = (sc_ref[0] + i) * bq
    has_pad = jnp.logical_and(first_row + bq == SEQ, txt_len < TXT)

    def scores(j):
        return lax.dot_general(k_ref[pl.ds(j * BK, BK), :], q_ref[...], NT, preferred_element_type=F32)

    def key_ok():
        return lax.broadcasted_iota(jnp.int32, (BK, 1), 0) < last + txt_len

    def finish(acc, l):
        o = acc * (1.0 / l)
        o_ref[...] = o.T.astype(BF)

        @pl.when(has_pad)
        def _():
            s = lax.dot_general(k_ref[pl.ds(VID, TXT), :], q_ref[...], NT, preferred_element_type=F32)
            pad_key = lax.broadcasted_iota(jnp.int32, (TXT, 1), 0) >= txt_len
            s = jnp.where(pad_key, s, -1e30)
            p = jnp.exp2(s - jnp.max(s, axis=0, keepdims=True))
            lp = jnp.sum(p, axis=0, keepdims=True)
            ap = jnp.dot(vt_ref[:, pl.ds(VID, TXT)], p.astype(BF), preferred_element_type=F32)
            row = first_row + lax.broadcasted_iota(jnp.int32, (bq, 1), 0)
            o_ref[...] = jnp.where(row < VID + txt_len, o_ref[...].astype(F32), (ap * (1.0 / lp)).T).astype(BF)

    @pl.when(flag_ref[0] == 1)
    def _():
        acc = jnp.zeros((HD, bq), F32)
        l = jnp.zeros((1, bq), F32)
        s = scores(0)
        for j in range(nk):
            nxt = scores(j + 1) if j + 1 < nk else None
            p = jnp.exp2(s)
            if j == nk - 1:
                p = jnp.where(key_ok(), p, 0.0)
            l = l + jnp.sum(p, axis=0, keepdims=True)
            acc = acc + jnp.dot(vt_ref[:, pl.ds(j * BK, BK)], p.astype(BF), preferred_element_type=F32)
            s = nxt
        finish(acc, l)

    @pl.when(flag_ref[0] == 0)
    def _():
        def step(j, carry):
            m, l, acc = carry
            at = pl.multiple_of(j * BK, BK)
            s = lax.dot_general(k_ref[pl.ds(at, BK), :], q_ref[...], NT, preferred_element_type=F32)
            s = jnp.where(jnp.logical_or(key_ok(), j < nk - 1), s, -1e30)
            mn = jnp.maximum(m, jnp.max(s, axis=0, keepdims=True))
            p = jnp.exp2(s - mn)
            a = jnp.exp2(m - mn)
            l = l * a + jnp.sum(p, axis=0, keepdims=True)
            acc = acc * a + jnp.dot(vt_ref[:, pl.ds(at, BK)], p.astype(BF), preferred_element_type=F32)
            return mn, l, acc

        init = (jnp.full((1, bq), -1e30, F32), jnp.zeros((1, bq), F32), jnp.zeros((HD, bq), F32))
        _, l, acc = lax.fori_loop(0, nk, step, init)
        finish(acc, l)


def attend(scalars, q, k, vt, rows, h0, nh):
    nb = rows // BQ
    return pl.pallas_call(
        attn_kernel,
        grid_spec=pltpu.PrefetchScalarGridSpec(
            num_scalar_prefetch=1, grid=(nh, nb),
            in_specs=[pl.BlockSpec((BQ, HD), lambda h, i, s: (s[0] + i, h0 + h)),
                      pl.BlockSpec((SEQ, HD), lambda h, i, s: (0, h0 + h)),
                      pl.BlockSpec((HD, SEQ), lambda h, i, s: (h0 + h, 0))],
            out_specs=pl.BlockSpec((BQ, HD), lambda h, i, s: (i, h)),
            scratch_shapes=[pltpu.SMEM((1,), jnp.int32)]),
        out_shape=jax.ShapeDtypeStruct((rows, nh * HD), BF), compiler_params=params(),
        cost_estimate=cost(6 * rows * SEQ * nh * HD, 4 * nh * HD * (SEQ + rows)), name="attend")(scalars, q, k, vt)


def gelu_kernel(half, nw, off_ref, y0_ref, y1_ref, *refs):
    w_refs, b_ref, o_ref = refs[:len(refs) - 2], refs[-2], refs[-1]
    bn = o_ref.shape[1]
    i = pl.program_id(0)
    j = pl.program_id(1)
    sub = 512 if bn % 512 == 0 else 768

    def step(y_ref, w_ref):
        for s in range(bn // sub):
            u = jnp.dot(y_ref[...], w_ref[:, pl.ds(s * sub, sub)], preferred_element_type=F32)
            u = u + b_ref[:, pl.ds(s * sub, sub)]
            h = 0.5 * u
            t = jnp.tanh(u * (0.7978845608028654 + 0.03567740813636141 * (u * u)))
            o_ref[:, pl.ds(s * sub, sub)] = (h * t + h).astype(BF)

    for a, y_ref in enumerate((y0_ref, y1_ref)):
        for c, w_ref in enumerate(w_refs):
            hit = (i < half) if a == 0 else (i >= half)
            if len(w_refs) > 1:
                hit = jnp.logical_and(hit, j // nw == c)

            @pl.when(hit)
            def _(y_ref=y_ref, w_ref=w_ref):
                step(y_ref, w_ref)


def mlp_in(off, ys, ws, b):
    n = ys[0].shape[0]
    f = sum(w.shape[1] for w in ws)
    bm = 768
    bn = 1024 if len(ws) == 1 else 768
    nw = ws[0].shape[1] // bn
    half = n // bm
    at = lambda i, o: jnp.where(i < half, o[0] + i, o[1] + i - half)
    wspec = lambda c: pl.BlockSpec((D, bn), lambda i, j, o: (0, jnp.clip(j - c * nw, 0, nw - 1)))
    return pl.pallas_call(
        functools.partial(gelu_kernel, half, nw),
        grid_spec=pltpu.PrefetchScalarGridSpec(
            num_scalar_prefetch=1, grid=(2 * half, f // bn),
            in_specs=[pl.BlockSpec((bm, D), lambda i, j, o: (jnp.minimum(i, half - 1), 0)),
                      pl.BlockSpec((bm, D), lambda i, j, o: (jnp.maximum(i - half, 0), 0))]
            + [wspec(c) for c in range(len(ws))] + [pl.BlockSpec((1, bn), lambda i, j, o: (0, j))],
            out_specs=pl.BlockSpec((bm, bn), lambda i, j, o: (at(i, o), j))),
        out_shape=jax.ShapeDtypeStruct((2 * n, f), BF),
        compiler_params=params(), cost_estimate=cost(4 * n * D * f, n * D * 4 + D * f * 2 + n * f * 4), name="mlp_in")(off, *ys, *ws, b)


def mm_kernel(x_ref, w_ref, o_ref):
    o_ref[...] = jnp.dot(x_ref[...], w_ref[...], preferred_element_type=F32)


def mm_f32(x, w):
    n, kd, f = x.shape[0], x.shape[1], w.shape[1]
    bm = bn = 1024
    return pl.pallas_call(
        mm_kernel, grid=(n // bm, f // bn),
        in_specs=[pl.BlockSpec((bm, kd), lambda i, j: (i, 0)), pl.BlockSpec((kd, bn), lambda i, j: (0, j))],
        out_specs=pl.BlockSpec((bm, bn), lambda i, j: (i, j)), out_shape=jax.ShapeDtypeStruct((n, f), F32),
        compiler_params=params(), cost_estimate=cost(2 * n * kd * f, n * kd * 2 + kd * f * 2 + n * f * 4), name="mlp_out")(x, w)


def out_kernel(final, off_ref, *refs):
    m_ref, wm0_ref, wm1_ref, a0_ref, a1_ref, b_ref, w0_ref, w1_ref, p_ref = refs[:9]
    o_ref = refs[-1]
    hk = wm0_ref.shape[0]
    dot = lambda a, w: jnp.dot(a, w, preferred_element_type=F32)
    acc = dot(m_ref[:, :hk], wm0_ref[...]) + dot(m_ref[:, hk:], wm1_ref[...])
    acc = acc + dot(a0_ref[...], w0_ref[...])
    acc = acc + dot(jnp.concatenate([a1_ref[...], b_ref[...]], axis=1), w1_ref[...])
    acc = acc + p_ref[...]
    if final:
        recv_ref, x_ref, gate_ref, bo_ref = refs[9:13]
        acc = x_ref[...].astype(F32) + gate_ref[...] * (acc + recv_ref[...] + bo_ref[...])
    o_ref[...] = acc.astype(o_ref.dtype)


def out_rows(off, n, m, wms, a0, a1s, w0, w1, part, tail=None):
    bm, bn = 768, 768
    f = D
    rowk = lambda kd: pl.BlockSpec((bm, kd), lambda i, j, o: (o[0] + i, 0))
    col = lambda kd: pl.BlockSpec((kd, bn), lambda i, j, o: (0, j))
    in_specs = [rowk(D), col(D // 2), col(D // 2), pl.BlockSpec((bm, DQ), lambda i, j, o: (i, 0)), rowk(DQ // 2), rowk(DQ // 2), col(DQ), col(DQ),
                pl.BlockSpec((bm, bn), lambda i, j, o: (o[0] + i, j))]
    args = [off, m, *wms, a0, *a1s, w0, w1, part]
    if tail is not None:
        tile = pl.BlockSpec((bm, bn), lambda i, j, o: (i, j))
        vec = pl.BlockSpec((1, bn), lambda i, j, o: (0, j))
        in_specs += [tile, tile, vec, vec]
        args += list(tail)
    dt = BF if tail is not None else F32
    return pl.pallas_call(
        functools.partial(out_kernel, tail is not None),
        grid_spec=pltpu.PrefetchScalarGridSpec(num_scalar_prefetch=1, grid=(n // bm, f // bn), in_specs=in_specs,
            out_specs=pl.BlockSpec((bm, bn), lambda i, j, o: (i, j))),
        out_shape=jax.ShapeDtypeStruct((n, f), dt), compiler_params=params(),
        cost_estimate=cost(2 * n * (D + 2 * DQ) * f, n * D * 14), name="out_rows")(*args)


def modulation(cond_vec, w_mod, b_mod):
    return jnp.dot(jax.nn.silu(cond_vec).astype(BF), w_mod, preferred_element_type=F32) + b_mod


def rope_table(grid_hw):
    n = lax.broadcasted_iota(jnp.int32, (SEQ, HD), 0)
    lane = lax.broadcasted_iota(jnp.int32, (SEQ, HD), 1)
    tok = lax.iota(jnp.int32, SEQ)
    gh = grid_hw[0, 0]
    gw = grid_hw[0, 1]
    t = (tok // (gh * gw)).astype(F32)
    r = ((tok // gw) % gh).astype(F32)
    c = (tok % gw).astype(F32)
    pair = lax.iota(jnp.int32, HD) // 2
    axis = (pair >= 8).astype(jnp.int32) + (pair >= 36).astype(jnp.int32)
    within = pair - jnp.where(axis == 0, 0, jnp.where(axis == 1, 8, 36))
    dim = jnp.where(axis == 0, 16.0, 56.0)
    freq = jnp.power(THETA, -2.0 * within.astype(F32) / dim)
    pos = jnp.where(axis[None] == 0, t[:, None], jnp.where(axis[None] == 1, r[:, None], c[:, None]))
    ang = jnp.where((tok < VID)[:, None], pos * freq[None], 0.0)
    sign = jnp.where(lax.iota(jnp.int32, HD) % 2 == 0, -1.0, 1.0)
    return jnp.cos(ang), jnp.sin(ang) * sign[None]


def pair_max(g):
    a = jnp.abs(g).reshape(HD // 2, 2)
    return jnp.max(a, axis=1)


def after(v, *deps):
    return lax.optimization_barrier((v,) + deps)[0]


def solution(mesh):
    def local_step(tokens, cond_vec, txt_len, grid_hw, w_mod, b_mod, w_qkv, b_qkv, q_gain, k_gain,
                   w_mlp_in, b_mlp_in, w_out_attn, w_out_mlp, b_out):
        tp = lax.axis_index('tp')
        dp = lax.axis_index('dp')
        chip = tp // 2
        own = tp % 2
        x = tokens[0]

        def swap_x(v):
            return lax.ppermute(v, 'tp', X_PAIRS)

        def swap_c(v):
            return lax.ppermute(v, 'tp', C_PAIRS)

        gather = lambda v: lax.all_gather(v, 'dp', axis=0, tiled=True)
        vec2 = lambda a, b: jnp.stack([a, b]).astype(jnp.int32)
        vec1 = lambda a: jnp.reshape(a, (1,)).astype(jnp.int32)

        q4 = D // 4
        hop_in = [swap_x(lax.dynamic_slice(w_mlp_in, (dp * q4, c * (D // 2)), (q4, D // 2))) for c in range(2)]
        hop_att = swap_x(lax.dynamic_slice_in_dim(w_out_attn, dp * (DQ // 4), DQ // 4, 0))
        hop_out = [swap_x(lax.dynamic_slice_in_dim(w_out_mlp, c * (D // 2) + dp * (D // 8), D // 8, 0)) for c in range(2)]
        b_in_o = swap_x(b_mlp_in)[None]

        mod = modulation(cond_vec, w_mod, b_mod)
        shift, scale, gate = mod[:, :D], mod[:, D:2 * D], mod[:, 2 * D:]
        y = norm(x, 1.0 + scale, shift)
        y_sib = swap_c(y)
        y_rem = swap_x(y)

        cos, sin = rope_table(grid_hw)
        w3 = jnp.transpose(w_qkv, (1, 0, 2))
        qg = (q_gain * (LOG2E * HD ** -0.5))[None]
        kg = k_gain[None]
        nb = SHARD // QBM
        sib = tp + 1 - 2 * own
        rem = (tp + 2) % 4
        remsib = (sib + 2) % 4
        tabs = (w3, b_qkv, qg, kg, cos, sin)
        rows2 = vec2(own * 2, 2 - own * 2)

        bufs = qkv(vec2(tp * nb, tp * nb), [y], *tabs)
        w_in_o0 = gather(after(hop_in[0], bufs[0]))
        m_own = mlp_in(rows2, [y, y_sib], [w_mlp_in], b_mlp_in[None])
        w_in_o1 = gather(after(hop_in[1], m_own))
        bufs = qkv(vec2(sib * nb, sib * nb), [y_sib], *tabs, bufs)
        part = mm_f32(m_own, w_out_mlp)
        w_att_o = gather(after(hop_att, part))
        m_oth = mlp_in(rows2, [y, y_sib], [w_in_o0, w_in_o1], b_in_o)
        y_rem = after(y_rem, m_oth)
        y_remsib = swap_c(y_rem)
        bufs = qkv(vec2(rem * nb, rem * nb), [y_rem], *tabs, bufs)
        w_out_o0 = gather(after(hop_out[0], bufs[0]))
        q, k, vt = qkv(vec2(remsib * nb, remsib * nb), [y_remsib], *tabs, bufs)

        gmax = jnp.max(pair_max(q_gain) * pair_max(k_gain)) * (HD ** 0.5 * LOG2E)
        ok = (gmax <= 96.0).astype(jnp.int32)
        sc = lambda b: jnp.stack([b, txt_len[0], ok]).astype(jnp.int32)
        att_r0 = attend(sc((1 - chip) * 2), q, k, vt, CHIP, 0, 3)
        att_b0 = swap_x(att_r0)
        w_out_o1 = gather(after(hop_out[1], att_r0))
        att_r1 = attend(after(sc((1 - chip) * 2), att_r0), q, k, vt, CHIP, 3, 3)
        att_b1 = swap_x(att_r1)
        att_s = attend(after(sc(sib), att_r1), q, k, vt, SHARD, 0, 6)

        weights = (w_out_attn, w_att_o)
        sib_part = out_rows(vec1((1 - own) * 2), SHARD, m_oth, (w_out_o0, w_out_o1), att_s, (att_b0, att_b1), *weights, part)
        recv = swap_c(sib_part)
        att_o = attend(after(sc(tp), sib_part), q, k, vt, SHARD, 0, 6)
        out = out_rows(vec1(own * 2), SHARD, m_oth, (w_out_o0, w_out_o1), att_o, (att_b0, att_b1), *weights, part,
                  (recv, x, gate, b_out[None]))
        return out[None]

    in_specs = (P('dp', 'tp', None), P('dp', None), P('dp'), P('dp', None), P(None, None), P(None), P(None, None, 'tp'), P(None, 'tp'), P(None), P(None), P(None, 'tp'), P('tp'), P('tp', None), P('tp', None), P(None))
    return jax.shard_map(local_step, mesh=mesh, in_specs=in_specs, out_specs=P('dp', 'tp', None), check_vma=False)
```

time: 3410 us -> 953 us (0.28)
  matrix products: 1280 us -> 19.9 us
  other arithmetic: 1250 us -> 21.9 us
  Pallas kernels: 0 us -> 696 us
  waiting for transfers between devices: 697 us -> 156 us
  local copies, waits for them, and re-layouts: 147 us -> 17.8 us
    dot_general x53 -> x1, matrix products: 1280 us -> 19.9 us  [modulation(): jnp.dot(jax.nn.silu(cond_vec).astype(BF), w_mod, preferred_element_type=F32)]
    sub x24 -> x0, other arithmetic: 994 us -> none  [one_block(): probs = jax.nn.softmax(scores, axis=-1).astype(jnp.bfloat16)]
    pallas_call x0 -> x14, Pallas kernels: none -> 696 us  [the longest x4 213 us: attend(): pl.pallas_call(attn_kernel, grid_spec=pltpu.PrefetchScalarGridSpec(num_sc...]
    reduce_scatter x1 -> x0, waiting for transfers between devices: 493 us -> none  [local_step(): own_sum = lax.psum_scatter(part_sum, 'tp', scatter_dimension=1, tiled=True)]
    all_gather x1 -> x5, waiting for transfers between devices: 204 us -> 0.06 us  [local_step(): gather = lambda v: lax.all_gather(v, 'dp', axis=0, tiled=True)]
    ppermute x0 -> x12, waiting for transfers between devices: none -> 156 us  [the longest x9 156 us: swap_x(): return lax.ppermute(v, 'tp', X_PAIRS)]
    another operation x27 -> x7, other arithmetic: 99.7 us -> 4.26 us  [the longest x4 2.41 us: local_step(): vec2 = lambda a, b: jnp.stack([a, b]).astype(jnp.int32)]
    mul x2 -> x1, other arithmetic: 66.2 us -> 13.9 us  [rope_table(): return (jnp.cos(ang), jnp.sin(ang) * sign[None])]
  transfers between devices with their start and end apart: 2 -> 17, of which waited for: 2 -> 2; matrix products, arithmetic and copies ran while one was open for 1% -> 5% of each run, Pallas kernels for 0% -> 62%
where the time goes in v1:
time: 953 us; the launch traced here: 939 us
  Pallas kernels  696 us (73%)
  waiting for transfers between devices  156 us (16%)
  other arithmetic  21.9 us (2%)
  matrix products  19.9 us (2%)
  between operations  19.4 us (2%)
  local copies, waits for them, and re-layouts  17.8 us (2%)
    pallas_call x4, Pallas kernels, attend(): pl.pallas_call(attn_kernel, grid_spec=pltpu.PrefetchScalarGridSpec(num_sc...  213 us
    pallas_call x2, Pallas kernels, mlp_in(): pl.pallas_call(functools.partial(gelu_kernel, half, nw), grid_spec=pltpu....  158 us
    ppermute x9, waiting for transfers between devices, swap_x(): return lax.ppermute(v, 'tp', X_PAIRS)  156 us
    pallas_call x4, Pallas kernels, qkv(): pl.pallas_call(functools.partial(qkv_kernel, half), grid_spec=pltpu.Prefe...  134 us
    pallas_call x2, Pallas kernels, out_rows(): pl.pallas_call(functools.partial(out_kernel, tail is not None), grid_spec...  112 us
    pallas_call x1, Pallas kernels, mm_f32(): pl.pallas_call(mm_kernel, grid=(n // bm, f // bn), in_specs=[pl.BlockSpec...  67.5 us
    dot_general x1, matrix products, modulation(): jnp.dot(jax.nn.silu(cond_vec).astype(BF), w_mod, preferred_element_type=F32)  19.9 us
  transfers between devices with their start and end apart: 17, of which 2 were waited for; matrix products, arithmetic and copies ran while one was open for 5% of the time, Pallas kernels for 62%

profile of v1, /device:TPU:0, one launch (start us, length us, event | category | flops | bytes accessed | tf_op | source)
XLA Modules:
  0.0 938.9 jit_solution(4276030663716257717)
XLA Ops:
  6.5 4.8 constant_dynamic-slice_fusion.4
  11.3 3.2 collective-permute-start.1
  14.5 19.9 %fusion.13 = f32[1,9216]{1,0:T(1,128)S(1)} fusion(bf16[3072,9216]{1,0:T(8,128)(2,1)} %param.19, f32[1,3072]{1,0:T(1,128)S(1)} %copy-done.5), kind=kOutput, calls=%fused_computation.26 | convolution fusion | flops 56638464 | bytes 56672256 | tf_op jit(solution)/shard_map/dot_general | solution.py:352
  35.1 11.4 %norm.1.y0_ref.y1_ref = bf16[1536,3072]{1,0:T(8,128)(2,1)} custom-call(bf16[1536,3072]{1,0:T(8,128)(2,1)} %bitcast.28, f32[1,3072]{1,0:T(1,128)} %get-tuple-element.55.scale_ref, f32[1,3072]{1,0:T(1,128)} %get-tuple-element.54.shift_ref), custom_call_target="tpu_custom_call" | custom-call | flops 37748736 | bytes 18874368 | tf_op jit(solution)/shard_map/norm/pallas_call | solution.py:48
  53.3 13.9 %sine_multiply_fusion = (f32[6144,128]{1,0:T(8,128)}, f32[6144,128]{1,0:T(8,128)}) fusion(f32[128]{0:T(128)S(1)} %get-tuple-element.60, f32[128]{0:T(128)S(1)} %get-tuple-element.61, f32[6144]{0:T(1024)S(1)} %get-tuple-element.67, f32[6144]{0:T(1024)S(1)} %get-tuple-element.66, f32[6144]{0:T(1024)S(1)} %fusion.1, pred[6144]{0:T(1024)(128)(4,1)S(1)} %iota_compare_fusion, ...), kind=kLoop, calls=%fused_computation | loop fusion | flops 3932160 | bytes 6372608 | tf_op jit(solution)/shard_map/mul | solution.py:372
  68.4 32.8 %qkv.4 = (bf16[6144,768]{1,0:T(8,128)(2,1)}, bf16[6144,768]{1,0:T(8,128)(2,1)}, bf16[768,6144]{1,0:T(8,128)(2,1)}) custom-call(s32[2]{0:T(128)} %pad_add_fusion.1.off_ref, bf16[1536,3072]{1,0:T(8,128)(2,1)} %norm.1.y0_ref.y1_ref, bf16[1536,3072]{1,0:T(8,128)(2,1)} %norm.1.y0_ref.y1_ref, bf16[3,3072,768]{2,1,0:T(8,128)(2,1)} %bitcast.32, f32[3,768]{1,0:T(4,128)} %b_ref.7, ...), custom_call_target="tpu_custom_call" | custom-call | flops 21743271936 | bytes 23592960 | tf_op jit(solution)/shard_map/qkv/pallas_call | solution.py:150
  103.3 78.5 %mlp_in.2.x_ref = bf16[3072,3072]{1,0:T(8,128)(2,1)} custom-call(s32[2]{0:T(128)} %pad_add_fusion.off_ref, bf16[1536,3072]{1,0:T(8,128)(2,1)} %norm.1.y0_ref.y1_ref, bf16[1536,3072]{1,0:T(8,128)(2,1)} %collective-permute-done.y1_ref.y0_ref, bf16[3072,3072]{1,0:T(8,128)(2,1)} %refs_0_.1, f32[1,3072]{1,0:T(1,128)} %bitcast.36), custom_call_target="tpu_custom_call" | custom-call | flops 57982058496 | bytes 56623104 | tf_op jit(solution)/shard_map/mlp_in/pallas_call | solution.py:288
  183.3 2.1 collective-permute-start.3
  186.7 2.0 collective-permute-start.10
  188.7 5.0 constant_dynamic-slice_fusion.1
  194.4 67.5 %mlp_out.1.refs_8_ = f32[3072,3072]{1,0:T(8,128)} custom-call(bf16[3072,3072]{1,0:T(8,128)(2,1)} %mlp_in.2.x_ref, bf16[3072,3072]{1,0:T(8,128)(2,1)} %w_ref.1), custom_call_target="tpu_custom_call" | custom-call | flops 57982058496 | bytes 75497472 | tf_op jit(solution)/shard_map/mlp_out/pallas_call | solution.py:307
  261.9 154.7 %collective-permute-done.10 = bf16[192,3072]{1,0:T(8,128)(2,1)S(1)} collective-permute-done((bf16[192,3072]{1,0:T(8,128)(2,1)S(1)}, bf16[192,3072]{1,0:T(8,128)(2,1)S(1)}, u32[]{:S(2)}, u32[]{:S(2)}) %collective-permute-start.10) | collective-permute-done | bytes 1179680 | tf_op jit(solution)/shard_map/ppermute | solution.py:394
  417.7 33.1 %qkv.5 = (bf16[6144,768]{1,0:T(8,128)(2,1)}, bf16[6144,768]{1,0:T(8,128)(2,1)}, bf16[768,6144]{1,0:T(8,128)(2,1)}) custom-call(s32[2]{0:T(128)} %get-tuple-element.63.off_ref, bf16[1536,3072]{1,0:T(8,128)(2,1)} %collective-permute-done.y1_ref.y0_ref, ...), custom_call_target="tpu_custom_call", output_to_operand_aliasing={{0}: (9, {}), {1}: (10, {}), {2}: (11, {})} | custom-call | flops 21743271936 | bytes 23592960 | tf_op jit(solution)/shard_map/qkv/pallas_call | solution.py:150
  451.4 80.0 %mlp_in.3.refs_0_ = bf16[3072,3072]{1,0:T(8,128)(2,1)} custom-call(s32[2]{0:T(128)} %pad_add_fusion.off_ref, bf16[1536,3072]{1,0:T(8,128)(2,1)} %norm.1.y0_ref.y1_ref, bf16[1536,3072]{1,0:T(8,128)(2,1)} %collective-permute-done.y1_ref.y0_ref, bf16[3072,1536]{1,0:T(8,128)(2,1)} %all-gather.6.cloned.1.call-done.refs_0_, ...), custom_call_target="tpu_custom_call" | custom-call | flops 57982058496 | bytes 56623104 | tf_op jit(solution)/shard_map/mlp_in/pallas_call | solution.py:288
  531.4 32.8 %qkv.6 = (bf16[6144,768]{1,0:T(8,128)(2,1)}, bf16[6144,768]{1,0:T(8,128)(2,1)}, bf16[768,6144]{1,0:T(8,128)(2,1)}) custom-call(s32[2]{0:T(128)} %get-tuple-element.62.off_ref, bf16[1536,3072]{1,0:T(8,128)(2,1)} %collective-permute-done.5.y0_ref.y1_ref, ...), custom_call_target="tpu_custom_call", output_to_operand_aliasing={{0}: (9, {}), {1}: (10, {}), {2}: (11, {})} | custom-call | flops 21743271936 | bytes 23592960 | tf_op jit(solution)/shard_map/qkv/pallas_call | solution.py:150
  568.2 34.9 %qkv.7 = (bf16[6144,768]{1,0:T(8,128)(2,1)}, bf16[6144,768]{1,0:T(8,128)(2,1)}, bf16[768,6144]{1,0:T(8,128)(2,1)}) custom-call(s32[2]{0:T(128)} %pad_add_fusion.4.off_ref, bf16[1536,3072]{1,0:T(8,128)(2,1)} %collective-permute-done.7.y0_ref.y1_ref, ...), custom_call_target="tpu_custom_call", output_to_operand_aliasing={{0}: (9, {}), {1}: (10, {}), {2}: (11, {})} | custom-call | flops 21743271936 | bytes 23592960 | tf_op jit(solution)/shard_map/qkv/pallas_call | solution.py:150
  603.1 54.9 %attend.4 = bf16[3072,384]{1,0:T(8,128)(2,1)} custom-call(s32[3]{0:T(128)} %add_add_fusion.sc_ref, bf16[6144,768]{1,0:T(8,128)(2,1)} %get-tuple-element.39.q_ref, bf16[6144,768]{1,0:T(8,128)(2,1)} %get-tuple-element.40.k_ref, bf16[768,6144]{1,0:T(8,128)(2,1)} %get-tuple-element.41.vt_ref), custom_call_target="tpu_custom_call" | custom-call | flops 43486543872 | bytes 14155776 | tf_op jit(solution)/shard_map/attend/pallas_call | solution.py:240
  658.6 53.9 %attend.5 = bf16[3072,384]{1,0:T(8,128)(2,1)} custom-call(s32[3]{0:T(128)} %add_add_fusion.sc_ref, bf16[6144,768]{1,0:T(8,128)(2,1)} %get-tuple-element.39.q_ref, bf16[6144,768]{1,0:T(8,128)(2,1)} %get-tuple-element.40.k_ref, bf16[768,6144]{1,0:T(8,128)(2,1)} %get-tuple-element.41.vt_ref), custom_call_target="tpu_custom_call" | custom-call | flops 43486543872 | bytes 14155776 | tf_op jit(solution)/shard_map/attend/pallas_call | solution.py:240
  712.5 52.4 %attend.6.refs_3_ = bf16[1536,768]{1,0:T(8,128)(2,1)} custom-call(s32[3]{0:T(128)} %add_add_fusion.2.sc_ref, bf16[6144,768]{1,0:T(8,128)(2,1)} %get-tuple-element.39.q_ref, bf16[6144,768]{1,0:T(8,128)(2,1)} %get-tuple-element.40.k_ref, bf16[768,6144]{1,0:T(8,128)(2,1)} %get-tuple-element.41.vt_ref), custom_call_target="tpu_custom_call" | custom-call | flops 43486543872 | bytes 23592960 | tf_op jit(solution)/shard_map/attend/pallas_call | solution.py:240
  765.0 1.5 collective-permute-done.9.refs_5_
  766.5 1.4 copy-done.8
  767.9 54.2 %out_rows.2 = f32[1536,3072]{1,0:T(8,128)} custom-call(s32[1]{0:T(128)} %bitcast.19.off_ref, bf16[3072,3072]{1,0:T(8,128)(2,1)} %mlp_in.3.refs_0_, bf16[1536,3072]{1,0:T(8,128)(2,1)} %all-gather.10.cloned.1.call-done.refs_1_, bf16[1536,3072]{1,0:T(8,128)(2,1)} %all-gather.12.cloned.1.call-done.refs_2_, bf16[1536,768]{1,0:T(8,128)(2,1)} %attend.6.refs_3_, ...), custom_call_target="tpu_custom_call" | custom-call | flops 43486543872 | bytes 66060288 | tf_op jit(solution)/shard_map/out_rows/pallas_call | solution.py:343
  822.7 52.0 %attend.7.refs_3_ = bf16[1536,768]{1,0:T(8,128)(2,1)} custom-call(s32[3]{0:T(128)} %add_add_fusion.1.sc_ref, bf16[6144,768]{1,0:T(8,128)(2,1)} %get-tuple-element.39.q_ref, bf16[6144,768]{1,0:T(8,128)(2,1)} %get-tuple-element.40.k_ref, bf16[768,6144]{1,0:T(8,128)(2,1)} %get-tuple-element.41.vt_ref), custom_call_target="tpu_custom_call" | custom-call | flops 43486543872 | bytes 23592960 | tf_op jit(solution)/shard_map/attend/pallas_call | solution.py:240
  874.8 57.4 %out_rows.3 = bf16[1536,3072]{1,0:T(8,128)(2,1)} custom-call(s32[1]{0:T(128)} %bitcast.off_ref, bf16[3072,3072]{1,0:T(8,128)(2,1)} %mlp_in.3.refs_0_, bf16[1536,3072]{1,0:T(8,128)(2,1)} %all-gather.10.cloned.1.call-done.refs_1_, bf16[1536,3072]{1,0:T(8,128)(2,1)} %all-gather.12.cloned.1.call-done.refs_2_, bf16[1536,768]{1,0:T(8,128)(2,1)} %attend.7.refs_3_, ...), custom_call_target="tpu_custom_call" | custom-call | flops 43486543872 | bytes 66060288 | tf_op jit(solution)/shard_map/out_rows/pallas_call | solution.py:343
  (82 shorter events, 15.2 us)
Async XLA Ops:
  6.5 444.3 %all-gather.6.cloned.1.call-start = ((), (), s32[]{:S(2)}) async-start(), calls=%async_computation | async-start | bytes 11796480 | tf_op jit(solution)/shard_map/all_gather | solution.py:399
  11.3 23.1 %copy-start.4 = (f32[9216]{0:T(1024)S(1)}, f32[9216]{0:T(1024)}, u32[]{:S(2)}) copy-start(f32[9216]{0:T(1024)} %param.20) | copy-start | bytes 110596
  11.3 89.9 %collective-permute-start.1 = (bf16[768,1536]{1,0:T(8,128)(2,1)}, bf16[768,1536]{1,0:T(8,128)(2,1)S(1)}, u32[]{:S(2)}, u32[]{:S(2)}) collective-permute-start(bf16[768,1536]{1,0:T(8,128)(2,1)} %get-tuple-element.50), channel_id=1, source_target_pairs={{0,2},{1,3},{2,0},{3,1},{4,6},{5,7},{6,4},{7,5},{8,10},{9,11},{10,... | collective-permute-start | bytes 7077896 | tf_op jit(solution)/shard_map/ppermute | solution.py:394
  35.1 11.4 %copy-start.6 = (s32[1,2]{1,0:T(1,128)S(1)}, s32[1,2]{1,0:T(1,128)}, u32[]{:S(2)}) copy-start(s32[1,2]{1,0:T(1,128)} %param.18) | copy-start | bytes 28
  46.5 21.3 %copy-start.11 = (f32[128]{0:T(128)S(1)}, f32[128]{0:T(128)}, u32[]{:S(2)}) copy-start(f32[128]{0:T(128)} %param.23) | copy-start | bytes 1540
  46.5 56.8 %collective-permute-start = (bf16[1536,3072]{1,0:T(8,128)(2,1)}, bf16[1536,3072]{1,0:T(8,128)(2,1)}, u32[]{:S(2)}, u32[]{:S(2)}) collective-permute-start(bf16[1536,3072]{1,0:T(8,128)(2,1)} %norm.1.y0_ref.y1_ref), channel_id=1, source_target_pairs={{0,1},{1,0},{2,3},{3,2},{4,5},{5,4},{6,7},{7,6},{8,9},{9,8},{10,11... | collective-permute-start | bytes 28311560 | tf_op jit(solution)/shard_map/ppermute | solution.py:397
  102.6 348.2 %all-gather.8.cloned.1.call-start = ((), (), s32[]{:S(2)}) async-start(), calls=%async_computation.1 | async-start | bytes 11796480 | tf_op jit(solution)/shard_map/all_gather | solution.py:399
  102.7 79.1 %collective-permute-start.2 = (bf16[768,1536]{1,0:T(8,128)(2,1)}, bf16[768,1536]{1,0:T(8,128)(2,1)S(1)}, u32[]{:S(2)}, u32[]{:S(2)}) collective-permute-start(bf16[768,1536]{1,0:T(8,128)(2,1)} %get-tuple-element.49), channel_id=1, source_target_pairs={{0,2},{1,3},{2,0},{3,1},{4,6},{5,7},{6,4},{7,5},{8,10},{9,11},{10,... | collective-permute-start | bytes 7077896 | tf_op jit(solution)/shard_map/ppermute | solution.py:394
  103.3 79.9 %copy-start.9 = (f32[3072]{0:T(1024)S(1)}, f32[3072]{0:T(1024)}, u32[]{:S(2)}) copy-start(f32[3072]{0:T(1024)} %param.26) | copy-start | bytes 36868
  183.2 581.8 %all-gather.14.cloned.1.call-start = ((), (), s32[]{:S(2)}) async-start(), calls=%async_computation.4 | async-start | bytes 5898240 | tf_op jit(solution)/shard_map/all_gather | solution.py:399
  183.3 267.5 %collective-permute-start.3 = (f32[3072]{0:T(1024)S(1)}, f32[3072]{0:T(1024)S(1)}, u32[]{:S(2)}, u32[]{:S(2)}) collective-permute-start(f32[3072]{0:T(1024)S(1)} %copy-done.9), channel_id=1, source_target_pairs={{0,2},{1,3},{2,0},{3,1},{4,6},{5,7},{6,4},{7,5},{8,10},{9,11},{10,... | collective-permute-start | bytes 36872 | tf_op jit(solution)/shard_map/ppermute | solution.py:394
  185.3 346.1 %collective-permute-start.5 = (bf16[1536,3072]{1,0:T(8,128)(2,1)}, bf16[1536,3072]{1,0:T(8,128)(2,1)}, u32[]{:S(2)}, u32[]{:S(2)}) collective-permute-start(bf16[1536,3072]{1,0:T(8,128)(2,1)} %norm.1.y0_ref.y1_ref), channel_id=1, source_target_pairs={{0,2},{1,3},{2,0},{3,1},{4,6},{5,7},{6,4},{7,5},{8,10},{9,11},{10,... | collective-permute-start | bytes 28311560 | tf_op jit(solution)/shard_map/ppermute | solution.py:394
  186.7 229.9 %collective-permute-start.10 = (bf16[192,3072]{1,0:T(8,128)(2,1)S(1)}, bf16[192,3072]{1,0:T(8,128)(2,1)S(1)}, u32[]{:S(2)}, u32[]{:S(2)}) collective-permute-start(bf16[192,3072]{1,0:T(8,128)(2,1)S(1)} %constant_dynamic-slice_fusion), channel_id=1, source_target_pairs={{0,2},{1,3},{2,0},{3,1},{4,6},{5,7},{6,4},{7,5},{8,10},{9,11},{10,... | collective-permute-start | bytes 3538952 | tf_op jit(solution)/shard_map/ppermute | solution.py:394
  193.7 370.6 %collective-permute-start.4 = (bf16[384,3072]{1,0:T(8,128)(2,1)}, bf16[384,3072]{1,0:T(8,128)(2,1)}, u32[]{:S(2)}, u32[]{:S(2)}) collective-permute-start(bf16[384,3072]{1,0:T(8,128)(2,1)} %get-tuple-element.48), channel_id=1, source_target_pairs={{0,2},{1,3},{2,0},{3,1},{4,6},{5,7},{6,4},{7,5},{8,10},{9,11},{10,... | collective-permute-start | bytes 7077896 | tf_op jit(solution)/shard_map/ppermute | solution.py:394
  417.7 348.8 %all-gather.10.cloned.1.call-start = ((), (), s32[]{:S(2)}) async-start(), calls=%async_computation.2 | async-start | bytes 11796480 | tf_op jit(solution)/shard_map/all_gather | solution.py:399
  531.4 36.8 %collective-permute-start.7 = (bf16[1536,3072]{1,0:T(8,128)(2,1)}, bf16[1536,3072]{1,0:T(8,128)(2,1)}, u32[]{:S(2)}, u32[]{:S(2)}) collective-permute-start(bf16[1536,3072]{1,0:T(8,128)(2,1)} %collective-permute-done.5.y0_ref.y1_ref), channel_id=1, source_target_pairs={{0,1},{1,0},{2,3},{3,2},{4,5},{5,4},{6,7},{7,6},{8,9},{9,8},{10,11... | collective-permute-start | bytes 28311560 | tf_op jit(solution)/shard_map/ppermute | solution.py:397
  531.4 33.0 %copy-start = (bf16[384,3072]{1,0:T(8,128)(2,1)S(1)}, bf16[384,3072]{1,0:T(8,128)(2,1)}, u32[]{:S(2)}) copy-start(bf16[384,3072]{1,0:T(8,128)(2,1)} %get-tuple-element.47) | copy-start | bytes 7077892
  531.4 33.0 %copy-start.12 = (f32[128]{0:T(128)S(1)}, f32[128]{0:T(128)}, u32[]{:S(2)}) copy-start(f32[128]{0:T(128)} %param.24) | copy-start | bytes 1540
  531.4 33.7 %copy-start.7 = (f32[128]{0:T(128)S(1)}, f32[128]{0:T(128)}, u32[]{:S(2)}) copy-start(f32[128]{0:T(128)} %get-tuple-element.56) | copy-start | bytes 1540
  564.3 202.1 %all-gather.12.cloned.1.call-start = ((), (), s32[]{:S(2)}) async-start(), calls=%async_computation.3 | async-start | bytes 11796480 | tf_op jit(solution)/shard_map/all_gather | solution.py:399
  564.4 93.6 %collective-permute-start.6 = (bf16[384,3072]{1,0:T(8,128)(2,1)S(1)}, bf16[384,3072]{1,0:T(8,128)(2,1)}, u32[]{:S(2)}, u32[]{:S(2)}) collective-permute-start(bf16[384,3072]{1,0:T(8,128)(2,1)S(1)} %copy-done), channel_id=1, source_target_pairs={{0,2},{1,3},{2,0},{3,1},{4,6},{5,7},{6,4},{7,5},{8,10},{9,11},{10,... | collective-permute-start | bytes 7077896 | tf_op jit(solution)/shard_map/ppermute | solution.py:394
  658.6 107.8 %collective-permute-start.8 = (bf16[3072,384]{1,0:T(8,128)(2,1)}, bf16[3072,384]{1,0:T(8,128)(2,1)S(1)}, u32[]{:S(2)}, u32[]{:S(2)}) collective-permute-start(bf16[3072,384]{1,0:T(8,128)(2,1)} %attend.4), channel_id=1, source_target_pairs={{0,2},{1,3},{2,0},{3,1},{4,6},{5,7},{6,4},{7,5},{8,10},{9,11},{10,... | collective-permute-start | bytes 7077896 | tf_op jit(solution)/shard_map/ppermute | solution.py:394
  712.5 53.9 %collective-permute-start.9 = (bf16[3072,384]{1,0:T(8,128)(2,1)}, bf16[3072,384]{1,0:T(8,128)(2,1)}, u32[]{:S(2)}, u32[]{:S(2)}) collective-permute-start(bf16[3072,384]{1,0:T(8,128)(2,1)} %attend.5), channel_id=1, source_target_pairs={{0,2},{1,3},{2,0},{3,1},{4,6},{5,7},{6,4},{7,5},{8,10},{9,11},{10,... | collective-permute-start | bytes 7077896 | tf_op jit(solution)/shard_map/ppermute | solution.py:394
  822.1 52.6 %collective-permute-start.11 = (f32[1536,3072]{1,0:T(8,128)}, f32[1536,3072]{1,0:T(8,128)}, u32[]{:S(2)}, u32[]{:S(2)}) collective-permute-start(f32[1536,3072]{1,0:T(8,128)} %out_rows.2), channel_id=1, source_target_pairs={{0,1},{1,0},{2,3},{3,2},{4,5},{5,4},{6,7},{7,6},{8,9},{9,8},{10,11... | collective-permute-start | bytes 56623112 | tf_op jit(solution)/shard_map/ppermute | solution.py:397
  (6 other events, 13.8 us)
Sparse Core Ops, SparseCore 0:
  102.8 92.7 all-gather.5
  197.3 92.4 all-gather.7
  417.8 53.4 all-gather.13
  564.4 92.7 all-gather.9
  658.9 92.4 all-gather.11

commit v2 on v0

v2 whole, which is shorter than its diff:
```python
import functools
import jax
import jax.numpy as jnp
import numpy as np
from jax import lax
from jax.experimental import pallas as pl
from jax.experimental.pallas import tpu as pltpu
from jax.sharding import PartitionSpec as P


SEQ = 6144
D = 3072
HD = 128
TXT = 256
VID = SEQ - TXT
EPS = 1e-6
THETA = 256.0
SHARD = 1536
CHIP = 2 * SHARD
DQ = 768
NH = DQ // HD
LOG2E = 1.4426950408889634
BF = jnp.bfloat16
F32 = jnp.float32
NT = (((1,), (1,)), ((), ()))
X_PAIRS = [(0, 2), (1, 3), (2, 0), (3, 1)]
C_PAIRS = [(0, 1), (1, 0), (2, 3), (3, 2)]


def params(mib=60, **kw):
    return pltpu.CompilerParams(vmem_limit_bytes=mib * 2 ** 20, **kw)


def cost(flops, nbytes):
    return pl.CostEstimate(flops=int(flops), bytes_accessed=int(nbytes), transcendentals=0)


PS = 12
MB = 3 * D // PS
RB = SEQ // PS
NB = SHARD // PS
YB = 256
FREQ = np.zeros((1, HD), np.float32)
for _l in range(HD):
    _p = _l // 2
    _d, _w = (16.0, _p) if _p < 8 else (56.0, _p - 8) if _p < 36 else (56.0, _p - 36)
    FREQ[0, _l] = np.float32(THETA) ** np.float32(-2.0 * _w / _d)


def prep_kernel(grid_ref, c_ref, wm_ref, bm_ref, x_ref, f_ref, qg_ref, kg_ref,
                y_ref, cos_ref, sin_ref, gate_ref, lim_ref, q_ref, k_ref, vt_ref, act_ref, mod_ref, nrm_ref):
    p = pl.program_id(0)

    @pl.when(p == 0)
    def _():
        c = c_ref[...]
        a = (c * jax.nn.sigmoid(c)).astype(BF)
        act_ref[...] = jnp.broadcast_to(a, (16, D))
        even = lax.broadcasted_iota(jnp.int32, (8, HD), 1) % 2 == 0

        def pair(g_ref):
            g = jnp.broadcast_to(jnp.abs(g_ref[...]), (8, HD))
            return jnp.maximum(g, jnp.where(even, pltpu.roll(g, HD - 1, 1), pltpu.roll(g, 1, 1)))

        bound = pair(qg_ref) * pair(kg_ref) * (HD ** 0.5 * LOG2E)
        lim_ref[...] = jnp.where(bound <= 96.0, 0.0, 1e30)

    @pl.when(p < PS)
    def _():
        m = jnp.dot(act_ref[...], wm_ref[...], preferred_element_type=F32)
        mod_ref[pl.ds(p, 1)] = (m[0:1] + bm_ref[...])[None]
        row = p * RB + lax.broadcasted_iota(jnp.int32, (RB, HD), 0)
        lane = lax.broadcasted_iota(jnp.int32, (1, HD), 1)
        n = row.astype(F32)
        gh = jnp.full((1, HD), grid_ref[0], jnp.int32).astype(F32)
        gw = jnp.full((1, HD), grid_ref[1], jnp.int32).astype(F32)
        line = jnp.floor((n + 0.5) * (1.0 / gw))
        frame = jnp.floor((line + 0.5) * (1.0 / gh))
        pos = jnp.where(lane < 16, frame, jnp.where(lane < 72, line - frame * gh, n - line * gw))
        ang = jnp.where(row < VID, pos * f_ref[...], 0.0)
        turn = jnp.floor(ang * 0.6366197723675814 + 0.5)
        r = ((ang - turn * 1.5703125) - turn * 4.837512969970703e-4) - turn * 7.549789954891882e-8
        z = r * r
        s = r + r * z * (-1.6666654611e-1 + z * (8.3321608736e-3 - z * 1.9515295891e-4))
        c = 1.0 - 0.5 * z + z * z * (4.166664568298827e-2 + z * (-1.388731625493765e-3 + z * 2.443315711809948e-5))
        t = turn.astype(jnp.int32)
        odd = (t & 1) == 1
        sv = jnp.where(odd, c, s)
        cv = jnp.where(odd, s, c)
        cos_ref[...] = jnp.where(((t + 1) & 2) == 2, -cv, cv)
        sin_ref[...] = jnp.where(((t & 2) == 2) != (lane % 2 == 0), -sv, sv)
        x = x_ref[...].astype(F32)
        d = x - jnp.mean(x, axis=-1, keepdims=True)
        var = jnp.mean(d * d, axis=-1, keepdims=True)
        nrm_ref[pl.ds(pl.multiple_of(p * NB, NB), NB), :] = d * lax.rsqrt(var + EPS)

    @pl.when(p == PS)
    def _():
        for j in range(PS // 3):
            gate_ref[0:1, pl.ds(j * MB, MB)] = mod_ref[2 * PS // 3 + j]

    @pl.when(p >= PS)
    def _():
        at = pl.multiple_of((p - PS) * YB, YB)
        for j in range(PS // 3):
            col = pl.ds(j * MB, MB)
            y_ref[:, col] = (nrm_ref[pl.ds(at, YB), col] * (1.0 + mod_ref[PS // 3 + j]) + mod_ref[j]).astype(BF)


def prep(grid_hw, cond, w_mod, b_mod, x, qg, kg):
    lo = lambda p: jnp.minimum(p, PS - 1)
    full = lambda *s: pl.BlockSpec(s, lambda p, g: (0,) * len(s))
    anyspec = pl.BlockSpec(memory_space=pl.ANY)
    return pl.pallas_call(
        prep_kernel,
        grid_spec=pltpu.PrefetchScalarGridSpec(
            num_scalar_prefetch=1, grid=(PS + SHARD // YB,),
            in_specs=[full(1, D), pl.BlockSpec((D, MB), lambda p, g: (0, lo(p))), pl.BlockSpec((1, MB), lambda p, g: (0, lo(p))),
                      pl.BlockSpec((NB, D), lambda p, g: (lo(p), 0)), full(1, HD), full(1, HD), full(1, HD)],
            out_specs=[pl.BlockSpec((YB, D), lambda p, g: (jnp.maximum(p - PS, 0), 0)),
                       pl.BlockSpec((RB, HD), lambda p, g: (lo(p), 0)), pl.BlockSpec((RB, HD), lambda p, g: (lo(p), 0)),
                       full(1, D), full(8, HD), anyspec, anyspec, anyspec],
            scratch_shapes=[pltpu.VMEM((16, D), BF), pltpu.VMEM((PS, 1, MB), F32), pltpu.VMEM((SHARD, D), F32)]),
        out_shape=[jax.ShapeDtypeStruct((SHARD, D), BF), jax.ShapeDtypeStruct((SEQ, HD), F32), jax.ShapeDtypeStruct((SEQ, HD), F32),
                   jax.ShapeDtypeStruct((1, D), F32), jax.ShapeDtypeStruct((8, HD), F32),
                   jax.ShapeDtypeStruct((SEQ, DQ), BF), jax.ShapeDtypeStruct((SEQ, DQ), BF), jax.ShapeDtypeStruct((DQ, SEQ), BF)],
        compiler_params=params(), cost_estimate=cost(2e10, 9e7), name="prep")(
            grid_hw.reshape(2), cond, w_mod, b_mod[None], x, FREQ, qg, kg)


QBM = 512
SUB = 256


def qkv_kernel(which_ref, sc_ref, y_ref, w_ref, b_ref, qg_ref, kg_ref, cos_ref, sin_ref, lim_in, _q, _k, _v,
               q_ref, k_ref, vt_ref, lim_ref, left0, left1):
    n = pl.program_id(1)
    tiles = [(i, s) for i in range(QBM // SUB) for s in range(DQ // SUB)]
    pairs = [tiles[a:a + 2] for a in range(0, len(tiles), 2)]

    @pl.when(jnp.logical_and(pl.program_id(0) == 0, n == 0))
    def _():
        lim_ref[...] = lim_in[...]

    def proj(t):
        return jnp.dot(y_ref[pl.ds(t[0] * SUB, SUB), :], w_ref[0, :, pl.ds(t[1] * SUB, SUB)], preferred_element_type=F32)

    def rope(r, t, gain, row, out_ref):
        at = pl.ds(t[0] * SUB, SUB)
        even = lax.broadcasted_iota(jnp.int32, (SUB, HD), 1) % 2 == 0
        for h in range(SUB // HD):
            lo = t[1] * SUB + h * HD
            x = r[:, h * HD:(h + 1) * HD] + b_ref[row:row + 1, lo:lo + HD]
            ms = jnp.mean(x * x, axis=-1, keepdims=True)
            x = x * lax.rsqrt(ms + EPS) * gain
            partner = jnp.where(even, pltpu.roll(x, HD - 1, 1), pltpu.roll(x, 1, 1))
            out_ref[at, lo:lo + HD] = (x * cos_ref[at, :] + partner * sin_ref[at, :]).astype(BF)

    def put(r, t):
        lo = t[1] * SUB
        v = r + b_ref[2:3, lo:lo + SUB]
        vt_ref[pl.ds(lo, SUB), pl.ds(t[0] * SUB, SUB)] = v.T.astype(BF)
        top = jnp.max(jnp.abs(v).reshape(SUB // 8, 8, SUB), axis=0)
        lim_ref[...] = jnp.maximum(lim_ref[...], jnp.maximum(top[:, :HD], top[:, HD:]))

    def q_epi(r, t):
        rope(r, t, qg_ref[...] * (LOG2E * HD ** -0.5), 0, q_ref)

    def k_epi(r, t):
        rope(r, t, kg_ref[...], 1, k_ref)

    def run(epi, before, keep):
        held = []
        for p, pair in enumerate(pairs):
            last = keep and p == len(pairs) - 1
            now = [(proj(t), t) for t in pair]
            if last:
                left0[...] = now[0][0]
                left1[...] = now[1][0]
            if p == 0 and before is not None:
                before(left0[...], pairs[-1][0])
                before(left1[...], pairs[-1][1])
            for r, t in held:
                epi(r, t)
            held = [] if last else now
        for r, t in held:
            epi(r, t)

    @pl.when(n == 0)
    def _():
        run(q_epi, None, True)

    @pl.when(n == 1)
    def _():
        run(k_epi, q_epi, True)

    @pl.when(n == 2)
    def _():
        run(put, k_epi, False)


def qkv(which, sc, y, w3, b, qg, kg, cos, sin, lim, bufs):
    m = SHARD // QBM
    at = lambda i, w, s: s[w[0]] * m + i
    full = lambda *s: pl.BlockSpec(s, lambda i, n, w, s_: (0,) * len(s))
    anyspec = pl.BlockSpec(memory_space=pl.ANY)
    return pl.pallas_call(
        qkv_kernel,
        grid_spec=pltpu.PrefetchScalarGridSpec(
            num_scalar_prefetch=2, grid=(m, 3),
            in_specs=[pl.BlockSpec((QBM, D), lambda i, n, w, s: (i, 0)),
                      pl.BlockSpec((1, D, DQ), lambda i, n, w, s: (n, 0, 0)),
                      full(3, DQ), full(1, HD), full(1, HD),
                      pl.BlockSpec((QBM, HD), lambda i, n, w, s: (at(i, w, s), 0)),
                      pl.BlockSpec((QBM, HD), lambda i, n, w, s: (at(i, w, s), 0)),
                      full(8, HD), anyspec, anyspec, anyspec],
            out_specs=[pl.BlockSpec((QBM, DQ), lambda i, n, w, s: (at(i, w, s), 0)),
                       pl.BlockSpec((QBM, DQ), lambda i, n, w, s: (at(i, w, s), 0)),
                       pl.BlockSpec((DQ, QBM), lambda i, n, w, s: (0, at(i, w, s))),
                       full(8, HD)],
            scratch_shapes=[pltpu.VMEM((SUB, SUB), F32)] * 2),
        out_shape=[jax.ShapeDtypeStruct((SEQ, DQ), BF), jax.ShapeDtypeStruct((SEQ, DQ), BF),
                   jax.ShapeDtypeStruct((DQ, SEQ), BF), jax.ShapeDtypeStruct((8, HD), F32)],
        input_output_aliases={10: 0, 11: 1, 12: 2}, compiler_params=params(),
        cost_estimate=cost(2 * SHARD * D * 3 * DQ, SHARD * D * 2 + 3 * D * DQ * 2), name="qkv")(
            which, sc, y, w3, b, qg, kg, cos, sin, lim, *bufs)


BQ = SHARD
BK = 512


def attn_kernel(head_ref, which_ref, row_ref, sc_ref, lim_ref, q_ref, k_ref, vt_ref, *refs):
    o_ref, flag_ref = refs[-2:]
    txt_len = sc_ref[4]

    @pl.when(pl.program_id(0) == 0)
    def _():
        flag_ref[0] = (jnp.max(lim_ref[...]) <= 4096.0).astype(jnp.int32)

    bq = q_ref.shape[0]
    nk = SEQ // BK
    last = BK - TXT
    first_row = sc_ref[which_ref[pl.program_id(0)]] * bq
    has_pad = jnp.logical_and(first_row + bq == SEQ, txt_len < TXT)

    def scores(j):
        return lax.dot_general(k_ref[pl.ds(j * BK, BK), :], q_ref[...], NT, preferred_element_type=F32)

    def key_ok():
        return lax.broadcasted_iota(jnp.int32, (BK, 1), 0) < last + txt_len

    def finish(acc, l):
        o = acc * (1.0 / l)
        o_ref[...] = o.T.astype(BF)

        @pl.when(has_pad)
        def _():
            s = lax.dot_general(k_ref[pl.ds(VID, TXT), :], q_ref[...], NT, preferred_element_type=F32)
            pad_key = lax.broadcasted_iota(jnp.int32, (TXT, 1), 0) >= txt_len
            s = jnp.where(pad_key, s, -1e30)
            p = jnp.exp2(s - jnp.max(s, axis=0, keepdims=True))
            lp = jnp.sum(p, axis=0, keepdims=True)
            ap = jnp.dot(vt_ref[:, pl.ds(VID, TXT)], p.astype(BF), preferred_element_type=F32)
            row = first_row + lax.broadcasted_iota(jnp.int32, (bq, 1), 0)
            o_ref[...] = jnp.where(row < VID + txt_len, o_ref[...].astype(F32), (ap * (1.0 / lp)).T).astype(BF)

    @pl.when(flag_ref[0] == 1)
    def _():
        acc = jnp.zeros((HD, bq), F32)
        l = jnp.zeros((1, bq), F32)
        s = scores(0)
        for j in range(nk):
            nxt = scores(j + 1) if j + 1 < nk else None
            p = jnp.exp2(s)
            if j == nk - 1:
                p = jnp.where(key_ok(), p, 0.0)
            l = l + jnp.sum(p, axis=0, keepdims=True)
            acc = acc + jnp.dot(vt_ref[:, pl.ds(j * BK, BK)], p.astype(BF), preferred_element_type=F32)
            s = nxt
        finish(acc, l)

    @pl.when(flag_ref[0] == 0)
    def _():
        def step(j, carry):
            m, l, acc = carry
            at = pl.multiple_of(j * BK, BK)
            s = lax.dot_general(k_ref[pl.ds(at, BK), :], q_ref[...], NT, preferred_element_type=F32)
            s = jnp.where(jnp.logical_or(key_ok(), j < nk - 1), s, -1e30)
            mn = jnp.maximum(m, jnp.max(s, axis=0, keepdims=True))
            p = jnp.exp2(s - mn)
            a = jnp.exp2(m - mn)
            l = l * a + jnp.sum(p, axis=0, keepdims=True)
            acc = acc * a + jnp.dot(vt_ref[:, pl.ds(at, BK)], p.astype(BF), preferred_element_type=F32)
            return mn, l, acc

        init = (jnp.full((1, bq), -1e30, F32), jnp.zeros((1, bq), F32), jnp.zeros((HD, bq), F32))
        _, l, acc = lax.fori_loop(0, nk, step, init)
        finish(acc, l)


def attend(pairs, blocks, sc, lim, q, k, vt, into=None):
    n = len(pairs)
    head, which, row = (np.array(v, np.int32) for v in zip(*(pairs + [pairs[-1]] * (16 - n))))
    in_specs = [pl.BlockSpec((8, HD), lambda i, h, w, r, s: (0, 0)),
                pl.BlockSpec((BQ, HD), lambda i, h, w, r, s: (s[w[i]], h[i])),
                pl.BlockSpec((SEQ, HD), lambda i, h, w, r, s: (0, h[i])),
                pl.BlockSpec((HD, SEQ), lambda i, h, w, r, s: (h[i], 0))]
    args = [head, which, row, sc, lim, q, k, vt]
    if into is not None:
        in_specs.append(pl.BlockSpec(memory_space=pl.ANY))
        args.append(into)
    return pl.pallas_call(
        attn_kernel,
        grid_spec=pltpu.PrefetchScalarGridSpec(
            num_scalar_prefetch=4, grid=(n,), in_specs=in_specs,
            out_specs=pl.BlockSpec((BQ, HD), lambda i, h, w, r, s: (r[i], h[i])),
            scratch_shapes=[pltpu.SMEM((1,), jnp.int32)]),
        out_shape=jax.ShapeDtypeStruct((blocks * BQ, DQ), BF), input_output_aliases={} if into is None else {8: 0},
        compiler_params=params(), cost_estimate=cost(6 * n * BQ * SEQ * HD, 4 * HD * n * (SEQ + BQ)), name="attend")(*args)


KC = 512
BN = 512
NL = BN // HD
NK = D // KC
NX = D // HD
NJ = D // BN
TILES = tuple((r, 256) for r in range(0, SHARD, 256))


def gelu(u):
    h = 0.5 * u
    t = jnp.tanh(u * (0.7978845608028654 + 0.03567740813636141 * (u * u)))
    return (h * t + h).astype(BF)


def dot(a, b):
    return jnp.dot(jnp.concatenate(a, axis=1), jnp.concatenate(b, axis=1), preferred_element_type=F32)


def tiled(product, store):
    held = None
    for tile in TILES:
        now = product(tile)
        if held is not None:
            store(*held)
        held = (tile, now)
    store(*held)


def started(copies):
    for c in copies:
        c.start()


def waited(copies):
    for c in copies:
        c.wait()


def mlp_kernel(fused, y0_ref, y1_ref, wa_ref, wb_ref, b_ref, o_ref, xs, ws, sx, sw, sf, *more):
    i = pl.program_id(0)
    s = pl.program_id(1)
    steps = 2 * NJ if fused else NJ
    slot = (i * steps + s) % 2

    def copy_x(y_ref, at, c):
        return [pltpu.make_async_copy(y_ref.at[:, pl.ds(x * HD, HD)], xs.at[at, x], sx.at[at, x]) for x in range(c * NL, c * NL + NL)]

    def columns(col, n):
        return pl.ds(pl.multiple_of(col * BN + n * HD, HD), HD)

    def copy_w(w_ref, col, at):
        return [pltpu.make_async_copy(w_ref.at[:, columns(col, n)], ws.at[at, n], sw.at[at, n]) for n in range(NL)]

    def first_w(c):
        k = pl.ds(c * KC, KC)
        return [pltpu.make_async_copy(wa_ref.at[k, columns(0, n)], ws.at[0, n, k], sf.at[c, n]) for n in range(NL)]

    first = jnp.logical_and(i == 0, s == 0)
    half = wa_ref.shape[1] // BN

    @pl.when(first)
    def _():
        for c in range(NK):
            started(copy_x(y0_ref, 0, c))
            started(first_w(c))

    @pl.when(s + 1 < half)
    def _():
        started(copy_w(wa_ref, s + 1, 1 - slot))

    @pl.when(jnp.logical_and(s + 1 >= half, s + 1 < steps))
    def _():
        started(copy_w(wb_ref, s + 1 - half, 1 - slot))

    @pl.when(jnp.logical_and(s + 1 == steps, i == 0))
    def _():
        started(copy_w(wa_ref, 0, 1 - slot))

    @pl.when(jnp.logical_and(s == 1, i == 0))
    def _():
        for c in range(NK):
            started(copy_x(y1_ref, 1, c))

    @pl.when(jnp.logical_and(s == 0, i == 1))
    def _():
        for c in range(NK):
            waited(copy_x(y1_ref, 1, c))

    bias = b_ref[:, pl.ds(pl.multiple_of(jnp.minimum(s, NJ - 1) * BN, BN), BN)]

    def put(tile, u):
        g = gelu(u + bias)
        if fused:
            for n in range(NL):
                more[0][s * NL + n, pl.ds(*tile), :] = g[:, n * HD:(n + 1) * HD]
        else:
            o_ref[pl.ds(*tile), :] = g

    @pl.when(first)
    def _():
        acc = [None] * len(TILES)
        for c in range(NK):
            waited(copy_x(y0_ref, 0, c))
            waited(first_w(c))
            w = [ws[0, n, pl.ds(c * KC, KC), :] for n in range(NL)]
            for n, tile in enumerate(TILES):
                r = dot([xs[0, x, pl.ds(*tile), :] for x in range(c * NL, c * NL + NL)], w)
                acc[n] = r if c == 0 else acc[n] + r
        for tile, u in zip(TILES, acc):
            put(tile, u)

    @pl.when(jnp.logical_not(first))
    def _():
        waited(copy_w(wa_ref, 0, slot))

    def weights():
        return [ws[slot, n] for n in range(NL)]

    @pl.when(jnp.logical_and(jnp.logical_not(first), s < NJ))
    def _():
        tiled(lambda tile: dot([xs[i, x, pl.ds(*tile), :] for x in range(NX)], weights()), put)

    if fused:
        @pl.when(s >= NJ)
        def _():
            def store(tile, r):
                o_ref[pl.ds(*tile), :] = r

            tiled(lambda tile: dot([more[0][x, pl.ds(*tile), :] for x in range(NX)], weights()), store)


def mlp(fused, y0, y1, wa, wb, b):
    steps = 2 * NJ if fused else NJ
    anyspec = pl.BlockSpec(memory_space=pl.ANY)
    dma = pltpu.SemaphoreType.DMA
    if fused:
        omap = lambda i, s: (jnp.where(s >= NJ, i, 0), jnp.where(s >= NJ, s - NJ, jnp.where(i == 0, 0, NJ - 1)))
    else:
        omap = lambda i, s: (i, s)
    scratch = [pltpu.VMEM((2, NX, SHARD, HD), BF), pltpu.VMEM((2, NL, D, HD), BF), dma((2, NX)), dma((2, NL)), dma((NK, NL))]
    return pl.pallas_call(
        functools.partial(mlp_kernel, fused), grid=(2, steps),
        in_specs=[anyspec] * 4 + [pl.BlockSpec((1, D), lambda i, s: (0, 0))],
        out_specs=pl.BlockSpec((SHARD, BN), omap), out_shape=jax.ShapeDtypeStruct((CHIP, D), F32 if fused else BF),
        scratch_shapes=scratch + ([pltpu.VMEM((NX, SHARD, HD), BF)] if fused else []),
        compiler_params=params(), cost_estimate=cost(2 * CHIP * D * steps * BN, CHIP * D * 8), name="mlp")(y0, y1, wa, wb, b)


KO = D + 2 * DQ
NP = 3
OCHUNKS = tuple((c * KC, KC) for c in range(NK)) + ((D, DQ), (D + DQ, DQ))


def out_kernel(final, first_row, a0_row, *refs):
    m_ref, *w_refs, a0_ref, a1_ref, v0_ref, v1_ref, p_ref = refs[:6 + NP]
    extra = refs[6 + NP:10 + NP] if final else ()
    o_ref, xs, ws, ps, sx, sw, sp = refs[6 + NP + len(extra):6 + NP + len(extra) + 7]
    j = pl.program_id(0)
    slot = j % 2
    if final:
        recv_ref, t_ref, gate_ref, bo_ref = extra
        rs, ts, sr, st = refs[-4:]

    def copy_x(c):
        k, n = OCHUNKS[c]
        cs = []
        for x in range(k // HD, (k + n) // HD):
            if k < D:
                s = m_ref.at[pl.ds(first_row, SHARD), pl.ds(x * HD, HD)]
            else:
                a_ref, row = (a0_ref, a0_row) if k == D else (a1_ref, 0)
                s = a_ref.at[pl.ds(row, SHARD), pl.ds(x * HD - k, HD)]
            cs.append(pltpu.make_async_copy(s, xs.at[x], sx.at[x]))
        return cs

    def copy_w(c, col, at):
        k, n = OCHUNKS[c]
        piece = D // NP
        w_ref, top = (w_refs[k // piece], k % piece) if k < D else (v0_ref, 0) if k == D else (v1_ref, 0)
        cols = lambda l: pl.ds(pl.multiple_of(col * BN + l * HD, HD), HD)
        return [pltpu.make_async_copy(w_ref.at[pl.ds(top, n), cols(l)], ws.at[at, l, pl.ds(k, n)], sw.at[at, c, l]) for l in range(NL)]

    def copy_tail(col, at):
        col = pl.ds(pl.multiple_of(col * BN, BN), BN)
        cs = [pltpu.make_async_copy(p_ref.at[pl.ds(first_row, SHARD), col], ps.at[at], sp.at[at])]
        if final:
            cs += [pltpu.make_async_copy(recv_ref.at[:, col], rs.at[at], sr.at[at]), pltpu.make_async_copy(t_ref.at[:, col], ts.at[at], st.at[at])]
        return cs

    chunks = range(len(OCHUNKS))

    @pl.when(j == 0)
    def _():
        for c in chunks:
            started(copy_x(c))
            started(copy_w(c, 0, 0))
        started(copy_tail(0, 0))

    @pl.when(j + 1 < NJ)
    def _():
        for c in chunks:
            started(copy_w(c, j + 1, 1 - slot))
        started(copy_tail(j + 1, 1 - slot))

    def store(tile, acc):
        rows = pl.ds(*tile)
        acc = acc + ps[slot, rows, :]
        if final:
            acc = ts[slot, rows, :].astype(F32) + gate_ref[...] * (acc + rs[slot, rows, :] + bo_ref[...])
        o_ref[rows, :] = acc.astype(o_ref.dtype)

    @pl.when(j == 0)
    def _():
        acc = [None] * len(TILES)
        for c in chunks:
            waited(copy_x(c))
            waited(copy_w(c, 0, 0))
            k, n = OCHUNKS[c]
            w = [ws[0, l, pl.ds(k, n), :] for l in range(NL)]
            for a, tile in enumerate(TILES):
                r = dot([xs[x, pl.ds(*tile), :] for x in range(k // HD, (k + n) // HD)], w)
                acc[a] = r if c == 0 else acc[a] + r
        waited(copy_tail(0, 0))
        for tile, r in zip(TILES, acc):
            store(tile, r)

    @pl.when(j > 0)
    def _():
        for c in chunks:
            waited(copy_w(c, 0, slot))
        waited(copy_tail(0, slot))
        tiled(lambda tile: dot([xs[x, pl.ds(*tile), :] for x in range(KO // HD)], [ws[slot, l] for l in range(NL)]), store)


def out_rows(first_row, a0_row, m, wms, a0, a1, v0, v1, part, tail=None):
    anyspec = pl.BlockSpec(memory_space=pl.ANY)
    vec = pl.BlockSpec((1, BN), lambda j: (0, j))
    final = tail is not None
    nc = len(OCHUNKS)
    dma = pltpu.SemaphoreType.DMA
    scratch = [pltpu.VMEM((KO // HD, SHARD, HD), BF), pltpu.VMEM((2, NL, KO, HD), BF), pltpu.VMEM((2, SHARD, BN), F32),
               dma((KO // HD,)), dma((2, nc, NL)), dma((2,))]
    if final:
        scratch += [pltpu.VMEM((2, SHARD, BN), F32), pltpu.VMEM((2, SHARD, BN), BF), dma((2,)), dma((2,))]
    return pl.pallas_call(
        functools.partial(out_kernel, final, first_row, a0_row), grid=(NJ,),
        in_specs=[anyspec] * (6 + NP) + ([anyspec, anyspec, vec, vec] if final else []),
        out_specs=pl.BlockSpec((SHARD, BN), lambda j: (0, j)),
        out_shape=jax.ShapeDtypeStruct((SHARD, D), BF if final else F32), scratch_shapes=scratch, compiler_params=params(),
        cost_estimate=cost(2 * SHARD * KO * D, SHARD * D * 14), name="out_rows")(m, *wms, a0, a1, v0, v1, part, *(tail or ()))


def after(v, *deps):
    return lax.optimization_barrier((v,) + deps)[0]


def solution(mesh):
    def local_step(tokens, cond_vec, txt_len, grid_hw, w_mod, b_mod, w_qkv, b_qkv, q_gain, k_gain,
                   w_mlp_in, b_mlp_in, w_out_attn, w_out_mlp, b_out):
        tp = lax.axis_index('tp')
        dp = lax.axis_index('dp')
        own = tp % 2
        x = tokens[0]

        def swap_x(v):
            return lax.ppermute(v, 'tp', X_PAIRS)

        def swap_c(v):
            return lax.ppermute(v, 'tp', C_PAIRS)

        gather = lambda v: lax.all_gather(v, 'dp', axis=0, tiled=True)

        q4 = D // 4
        split = D // 3
        hop_in = [swap_x(lax.dynamic_slice(w_mlp_in, (dp * q4, lo), (q4, n)))
                  for lo, n in ((0, split), (split, D - split))]
        hop_att = swap_x(lax.dynamic_slice_in_dim(w_out_attn, dp * (DQ // 4), DQ // 4, 0))
        hop_out = [swap_x(lax.dynamic_slice_in_dim(w_out_mlp, c * split + dp * (split // 4), split // 4, 0)) for c in range(NP)]
        b_in_o = swap_x(b_mlp_in)[None]

        sib = tp + 1 - 2 * own
        rem = (tp + 2) % 4
        remsib = (sib + 2) % 4
        sc = jnp.stack([tp, sib, rem, remsib, txt_len[0]]).astype(jnp.int32)
        OWN, SIB, REM, REMSIB = (np.full((1,), i, np.int32) for i in range(4))

        qg = q_gain[None]
        kg = k_gain[None]
        y, cos, sin, gate, lim, *bufs = prep(grid_hw, cond_vec, w_mod, b_mod, x, qg, kg)
        y_sib = swap_c(y)
        y_rem = swap_x(y)
        tabs = (jnp.transpose(w_qkv, (1, 0, 2)), b_qkv, qg, kg, cos, sin)

        w_in_o0 = gather(after(hop_in[0], y))
        *bufs, lim = qkv(OWN, sc, y, *tabs, lim, bufs)
        *bufs, lim = qkv(SIB, sc, y_sib, *tabs, lim, bufs)
        w_in_o1 = gather(after(hop_in[1], lim))
        part = mlp(True, y, after(y_sib, lim), w_mlp_in, w_out_mlp, b_mlp_in[None])
        w_att_o = gather(after(hop_att, part))
        m_oth = mlp(False, y, y_sib, w_in_o0, w_in_o1, b_in_o)
        y_rem = after(y_rem, m_oth)
        y_remsib = swap_c(y_rem)
        *bufs, lim = qkv(REM, sc, y_rem, *tabs, lim, bufs)
        w_out_o = [gather(after(hop_out[0], lim))]
        q, k, vt, lim = qkv(REMSIB, sc, y_remsib, *tabs, lim, bufs)
        w_out_o.append(gather(after(hop_out[1], lim)))

        att_r0 = attend([(h, 3, 0) for h in range(NH)], 1, sc, lim, q, k, vt)
        att_b0 = swap_x(att_r0)
        w_out_o.append(gather(after(hop_out[2], att_r0)))
        att_r1 = attend([(h, 2, 0) for h in range(NH)], 1, after(sc, att_r0), lim, q, k, vt)
        att_b1 = swap_x(att_r1)
        some = NH // 2
        att_a = attend([(h, 1, 0) for h in range(NH)] + [(h, 0, 1) for h in range(some)], 2, after(sc, att_r1), lim, q, k, vt)

        wms = tuple(w_out_o)
        weights = (w_out_attn, w_att_o, part)
        sib_part = out_rows(SHARD, 0, m_oth, wms, att_a, att_b0, *weights)
        recv = swap_c(sib_part)
        att_a = attend([(h, 0, 1) for h in range(some, NH)], 2, after(sc, sib_part), lim, q, k, vt, after(att_a, sib_part))
        out = out_rows(0, SHARD, m_oth, wms, att_a, att_b1, *weights, (recv, x, gate, b_out[None]))
        return out[None]

    in_specs = (P('dp', 'tp', None), P('dp', None), P('dp'), P('dp', None), P(None, None), P(None), P(None, None, 'tp'), P(None, 'tp'), P(None), P(None), P(None, 'tp'), P('tp'), P('tp', None), P('tp', None), P(None))
    return jax.shard_map(local_step, mesh=mesh, in_specs=in_specs, out_specs=P('dp', 'tp', None), check_vma=False)
```

time: 3410 us -> 902 us (0.26)
  matrix products: 1280 us -> 0 us
  other arithmetic: 1250 us -> 0 us
  Pallas kernels: 0 us -> 693 us
  waiting for transfers between devices: 697 us -> 146 us
  local copies, waits for them, and re-layouts: 147 us -> 21 us
    dot_general x53 -> x0, matrix products: 1280 us -> none  [the longest x24 434 us: one_block(): jnp.einsum('bhqk,bkhd->bqhd', probs, v_heads, preferred_element_type=jnp....]
    sub x24 -> x0, other arithmetic: 994 us -> none  [one_block(): probs = jax.nn.softmax(scores, axis=-1).astype(jnp.bfloat16)]
    pallas_call x0 -> x13, Pallas kernels: none -> 693 us  [the longest x4 210 us: attend(): pl.pallas_call(attn_kernel, grid_spec=pltpu.PrefetchScalarGridSpec(num_sc...]
    reduce_scatter x1 -> x0, waiting for transfers between devices: 493 us -> none  [local_step(): own_sum = lax.psum_scatter(part_sum, 'tp', scatter_dimension=1, tiled=True)]
    all_gather x1 -> x6, waiting for transfers between devices: 204 us -> 0.09 us  [local_step(): gather = lambda v: lax.all_gather(v, 'dp', axis=0, tiled=True)]
    ppermute x0 -> x13, waiting for transfers between devices: none -> 146 us  [the longest x10 146 us: swap_x(): return lax.ppermute(v, 'tp', X_PAIRS)]
    another operation x27 -> x0, other arithmetic: 99.7 us -> none
    mul x2 -> x0, other arithmetic: 66.2 us -> none  [the longest x1 36.1 us: head_rms(): mean_sq = jnp.mean(heads_f32 * heads_f32, axis=-1, keepdims=True)]
  transfers between devices with their start and end apart: 2 -> 19, of which waited for: 2 -> 4; matrix products, arithmetic and copies ran while one was open for 1% -> 2% of each run, Pallas kernels for 0% -> 62%
where the time goes in v2:
time: 902 us; the launch traced here: 894 us
  Pallas kernels  693 us (77%)
  waiting for transfers between devices  146 us (16%)
  local copies, waits for them, and re-layouts  21 us (2%)
  starting transfers between devices  19.2 us (2%)
  between operations  14.5 us (2%)
    pallas_call x4, Pallas kernels, attend(): pl.pallas_call(attn_kernel, grid_spec=pltpu.PrefetchScalarGridSpec(num_sc...  210 us
    pallas_call x2, Pallas kernels, mlp(): pl.pallas_call(functools.partial(mlp_kernel, fused), grid=(2, steps), in_...  207 us
    ppermute x10, waiting for transfers between devices, swap_x(): return lax.ppermute(v, 'tp', X_PAIRS)  146 us
    pallas_call x4, Pallas kernels, qkv(): pl.pallas_call(qkv_kernel, grid_spec=pltpu.PrefetchScalarGridSpec(num_sca...  134 us
    pallas_call x2, Pallas kernels, out_rows(): pl.pallas_call(functools.partial(out_kernel, final, first_row, a0_row), g...  108 us
    pallas_call x1, Pallas kernels, prep(): pl.pallas_call(prep_kernel, grid_spec=pltpu.PrefetchScalarGridSpec(num_sc...  34.7 us
    ppermute x10, starting transfers between devices, swap_x(): return lax.ppermute(v, 'tp', X_PAIRS)  18.2 us
  transfers between devices with their start and end apart: 19, of which 4 were waited for; matrix products, arithmetic and copies ran while one was open for 2% of the time, Pallas kernels for 62%

profile of v2, /device:TPU:0, one launch (start us, length us, event | category | flops | bytes accessed | tf_op | source)
XLA Modules:
  0.0 894.2 jit_solution(408131897889033517)
XLA Ops:
  6.5 34.7 %prep.1 = (bf16[1536,3072]{1,0:T(8,128)(2,1)}, f32[6144,128]{1,0:T(8,128)}, f32[6144,128]{1,0:T(8,128)}, f32[1,3072]{1,0:T(1,128)}, f32[8,128]{1,0:T(8,128)}, /*...) custom-call(s32[2]{0:T(128)} %bitcast.24, f32[1,3072]{1,0:T(1,128)} %c_ref.1, ...), custom_call_target="tpu_custom_call" | custom-call | flops 20000000000 | bytes 90000000 | tf_op jit(solution)/shard_map/prep/pallas_call | solution.py:114
  42.0 1.5 constant_dynamic-slice_fusion.4
  43.5 2.5 collective-permute-start.1
  46.0 35.0 %collective-permute-done.1 = bf16[768,1024]{1,0:T(8,128)(2,1)S(1)} collective-permute-done((bf16[768,1024]{1,0:T(8,128)(2,1)S(1)}, bf16[768,1024]{1,0:T(8,128)(2,1)S(1)}, u32[]{:S(2)}, u32[]{:S(2)}) %collective-permute-start.1) | collective-permute-done | bytes 1572896 | tf_op jit(solution)/shard_map/ppermute | solution.py:589
  82.4 4.0 constant_dynamic-slice_fusion.5
  86.4 1.7 collective-permute-start.2
  89.4 34.2 %qkv.4 = (bf16[6144,768]{1,0:T(8,128)(2,1)}, bf16[6144,768]{1,0:T(8,128)(2,1)}, bf16[768,6144]{1,0:T(8,128)(2,1)}, f32[8,128]{1,0:T(8,128)}) custom-call(s32[1]{0:T(128)} %constant.81.clone.which_ref, s32[5]{0:T(128)} %stack.19.sc_ref, ...), custom_call_target="tpu_custom_call", output_to_operand_aliasing={{0}: (10, {}), {1}: (11, {}), {2}: (12, {})} | custom-call | flops 21743271936 | bytes 23592960 | tf_op jit(solution)/shard_map/qkv/pallas_call | solution.py:207
  123.7 32.8 %qkv.5 = (bf16[6144,768]{1,0:T(8,128)(2,1)}, bf16[6144,768]{1,0:T(8,128)(2,1)}, bf16[768,6144]{1,0:T(8,128)(2,1)}, f32[8,128]{1,0:T(8,128)}) custom-call(s32[1]{0:T(128)} %constant.82.clone.which_ref, s32[5]{0:T(128)} %stack.19.sc_ref, ...), custom_call_target="tpu_custom_call", output_to_operand_aliasing={{0}: (10, {}), {1}: (11, {}), {2}: (12, {})} | custom-call | flops 21743271936 | bytes 23592960 | tf_op jit(solution)/shard_map/qkv/pallas_call | solution.py:207
  156.5 1.7 copy-done
  163.2 5.7 constant_dynamic-slice_fusion.1
  169.1 135.4 %mlp.3.refs_8_ = f32[3072,3072]{1,0:T(8,128)} custom-call(bf16[1536,3072]{1,0:T(8,128)(2,1)} %get-tuple-element.41.y_ref.y0_ref, bf16[1536,3072]{1,0:T(8,128)(2,1)} %collective-permute-done.y_ref.y1_ref, bf16[3072,3072]{1,0:T(8,128)(2,1)} %wa_ref.1, bf16[3072,3072]{1,0:T(8,128)(2,1)} %wb_ref.1, f32[1,3072]{1,0:T(1,128)} %bitcast.21), custom_call_target="tpu_custom_call" | custom-call | flops 115964116992 | bytes 75497472 | tf_op jit(solution)/shard_map/mlp/pallas_call | solution.py:464
  304.6 85.3 %collective-permute-done.10 = bf16[192,3072]{1,0:T(8,128)(2,1)S(1)} collective-permute-done((bf16[192,3072]{1,0:T(8,128)(2,1)S(1)}, bf16[192,3072]{1,0:T(8,128)(2,1)S(1)}, u32[]{:S(2)}, u32[]{:S(2)}) %collective-permute-start.10) | collective-permute-done | bytes 1179680 | tf_op jit(solution)/shard_map/ppermute | solution.py:589
  391.6 71.6 %mlp.2.refs_0_ = bf16[3072,3072]{1,0:T(8,128)(2,1)} custom-call(bf16[1536,3072]{1,0:T(8,128)(2,1)} %get-tuple-element.41.y_ref.y0_ref, bf16[1536,3072]{1,0:T(8,128)(2,1)} %collective-permute-done.y_ref.y1_ref, bf16[3072,1024]{1,0:T(8,128)(2,1)} %all-gather.7.cloned.1.call-done.wa_ref, bf16[3072,2048]{1,0:T(8,128)(2,1)} %all-gather.9.cloned.1.call-done.wb_ref, ...), custom_call_target="tpu_custom_call" | custom-call | flops 57982058496 | bytes 75497472 | tf_op jit(solution)/shard_map/mlp/pallas_call | solution.py:464
  463.3 33.0 %qkv.6 = (bf16[6144,768]{1,0:T(8,128)(2,1)}, bf16[6144,768]{1,0:T(8,128)(2,1)}, bf16[768,6144]{1,0:T(8,128)(2,1)}, f32[8,128]{1,0:T(8,128)}) custom-call(s32[1]{0:T(128)} %constant.83.clone.which_ref, s32[5]{0:T(128)} %stack.19.sc_ref, ...), custom_call_target="tpu_custom_call", output_to_operand_aliasing={{0}: (10, {}), {1}: (11, {}), {2}: (12, {})} | custom-call | flops 21743271936 | bytes 23592960 | tf_op jit(solution)/shard_map/qkv/pallas_call | solution.py:207
  497.9 33.9 %qkv.7 = (bf16[6144,768]{1,0:T(8,128)(2,1)}, bf16[6144,768]{1,0:T(8,128)(2,1)}, bf16[768,6144]{1,0:T(8,128)(2,1)}, f32[8,128]{1,0:T(8,128)}) custom-call(s32[1]{0:T(128)} %constant.84.clone.which_ref, s32[5]{0:T(128)} %stack.19.sc_ref, ...), custom_call_target="tpu_custom_call", output_to_operand_aliasing={{0}: (10, {}), {1}: (11, {}), {2}: (12, {})} | custom-call | flops 21743271936 | bytes 23592960 | tf_op jit(solution)/shard_map/qkv/pallas_call | solution.py:207
  531.8 1.5 collective-permute-done.6
  535.9 56.1 %attend.4 = bf16[1536,768]{1,0:T(8,128)(2,1)} custom-call(s32[16]{0:T(128)} %constant.85.clone.head_ref, s32[16]{0:T(128)} %call_exported.0.which_ref, s32[16]{0:T(128)} %call_exported.1.row_ref.which_ref, s32[5]{0:T(128)} %stack.19.sc_ref, f32[8,128]{1,0:T(8,128)} %get-tuple-element.64.lim_ref, bf16[6144,768]{1,0:T(8,128)(2,1)} %get-tuple-element.66.q_ref, ...), custom_call_target="tpu_custom_call" | custom-call | flops 43486543872 | bytes 23592960 | tf_op jit(solution)/shard_map/attend/pallas_call | solution.py:313
  593.7 52.1 %attend.5 = bf16[1536,768]{1,0:T(8,128)(2,1)} custom-call(s32[16]{0:T(128)} %constant.85.clone.head_ref, s32[16]{0:T(128)} %call_exported.2.which_ref, s32[16]{0:T(128)} %call_exported.1.row_ref.which_ref, s32[5]{0:T(128)} %stack.19.sc_ref, f32[8,128]{1,0:T(8,128)} %get-tuple-element.64.lim_ref, bf16[6144,768]{1,0:T(8,128)(2,1)} %get-tuple-element.66.q_ref, ...), custom_call_target="tpu_custom_call" | custom-call | flops 43486543872 | bytes 23592960 | tf_op jit(solution)/shard_map/attend/pallas_call | solution.py:313
  645.8 74.3 %attend.6.refs_4_.refs_0_ = bf16[3072,768]{1,0:T(8,128)(2,1)} custom-call(s32[16]{0:T(128)} %constant.89.clone.head_ref, s32[16]{0:T(128)} %constant.90.clone.which_ref, s32[16]{0:T(128)} %constant.91.clone.row_ref, s32[5]{0:T(128)} %stack.19.sc_ref, f32[8,128]{1,0:T(8,128)} %get-tuple-element.64.lim_ref, bf16[6144,768]{1,0:T(8,128)(2,1)} %get-tuple-element.66.q_ref, ...), custom_call_target="tpu_custom_call" | custom-call | flops 65229815808 | bytes 35389440 | tf_op jit(solution)/shard_map/attend/pallas_call | solution.py:313
  720.2 52.9 %out_rows.2 = f32[1536,3072]{1,0:T(8,128)} custom-call(bf16[3072,3072]{1,0:T(8,128)(2,1)} %mlp.2.refs_0_, bf16[1024,3072]{1,0:T(8,128)(2,1)} %all-gather.11.cloned.1.call-done.refs_1_, bf16[1024,3072]{1,0:T(8,128)(2,1)} %all-gather.13.cloned.1.call-done.refs_2_, bf16[1024,3072]{1,0:T(8,128)(2,1)} %all-gather.15.cloned.1.call-done.refs_3_, ...), custom_call_target="tpu_custom_call" | custom-call | flops 43486543872 | bytes 66060288 | tf_op jit(solution)/shard_map/out_rows/pallas_call | solution.py:568
  773.2 7.2 collective-permute-start.11
  780.9 27.2 %attend.7.refs_4_ = bf16[3072,768]{1,0:T(8,128)(2,1)} custom-call(s32[16]{0:T(128)} %constant.92.clone.head_ref, s32[16]{0:T(128)} %call_exported.1.row_ref.which_ref, s32[16]{0:T(128)} %call_exported.3.row_ref, s32[5]{0:T(128)} %stack.19.sc_ref, f32[8,128]{1,0:T(8,128)} %get-tuple-element.64.lim_ref, ...), custom_call_target="tpu_custom_call", output_to_operand_aliasing={{}: (8, {})} | custom-call | flops 21743271936 | bytes 11796480 | tf_op jit(solution)/shard_map/attend/pallas_call | solution.py:313
  808.1 24.2 %collective-permute-done.11.refs_5_ = bf16[1536,768]{1,0:T(8,128)(2,1)} collective-permute-done((bf16[1536,768]{1,0:T(8,128)(2,1)S(1)}, bf16[1536,768]{1,0:T(8,128)(2,1)}, u32[]{:S(2)}, u32[]{:S(2)}) %collective-permute-start.11) | collective-permute-done | bytes 2359328 | tf_op jit(solution)/shard_map/ppermute | solution.py:589
  832.3 54.8 %out_rows.3 = bf16[1536,3072]{1,0:T(8,128)(2,1)} custom-call(bf16[3072,3072]{1,0:T(8,128)(2,1)} %mlp.2.refs_0_, bf16[1024,3072]{1,0:T(8,128)(2,1)} %all-gather.11.cloned.1.call-done.refs_1_, bf16[1024,3072]{1,0:T(8,128)(2,1)} %all-gather.13.cloned.1.call-done.refs_2_, bf16[1024,3072]{1,0:T(8,128)(2,1)} %all-gather.15.cloned.1.call-done.refs_3_, ...), custom_call_target="tpu_custom_call" | custom-call | flops 43486543872 | bytes 66060288 | tf_op jit(solution)/shard_map/out_rows/pallas_call | solution.py:568
  (60 shorter events, 16.0 us)
Async XLA Ops:
  6.5 384.5 %all-gather.7.cloned.1.call-start = ((), (), s32[]{:S(2)}) async-start(), calls=%async_computation | async-start | bytes 7864320 | tf_op jit(solution)/shard_map/all_gather | solution.py:594
  41.2 82.4 %collective-permute-start = (bf16[1536,3072]{1,0:T(8,128)(2,1)}, bf16[1536,3072]{1,0:T(8,128)(2,1)}, u32[]{:S(2)}, u32[]{:S(2)}) collective-permute-start(bf16[1536,3072]{1,0:T(8,128)(2,1)} %get-tuple-element.41.y_ref.y0_ref), channel_id=1, source_target_pairs={{0,1},{1,0},{2,3},{3,2},{4,5},{5,4},{6,7},{7,6},{8,9},{9,8},{10,11... | collective-permute-start | bytes 28311560 | tf_op jit(solution)/shard_map/ppermute | solution.py:592
  43.5 37.6 %collective-permute-start.1 = (bf16[768,1024]{1,0:T(8,128)(2,1)S(1)}, bf16[768,1024]{1,0:T(8,128)(2,1)S(1)}, u32[]{:S(2)}, u32[]{:S(2)}) collective-permute-start(bf16[768,1024]{1,0:T(8,128)(2,1)S(1)} %constant_dynamic-slice_fusion.4), channel_id=1, source_target_pairs={{0,2},{1,3},{2,0},{3,1},{4,6},{5,7},{6,4},{7,5},{8,10},{9,11},{10,... | collective-permute-start | bytes 4718600 | tf_op jit(solution)/shard_map/ppermute | solution.py:589
  82.3 308.7 %all-gather.9.cloned.1.call-start = ((), (), s32[]{:S(2)}) async-start(), calls=%async_computation.1 | async-start | bytes 15728640 | tf_op jit(solution)/shard_map/all_gather | solution.py:594
  86.4 70.2 %collective-permute-start.2 = (bf16[768,2048]{1,0:T(8,128)(2,1)}, bf16[768,2048]{1,0:T(8,128)(2,1)S(1)}, u32[]{:S(2)}, u32[]{:S(2)}) collective-permute-start(bf16[768,2048]{1,0:T(8,128)(2,1)} %constant_dynamic-slice_fusion.5), channel_id=1, source_target_pairs={{0,2},{1,3},{2,0},{3,1},{4,6},{5,7},{6,4},{7,5},{8,10},{9,11},{10,... | collective-permute-start | bytes 9437192 | tf_op jit(solution)/shard_map/ppermute | solution.py:589
  123.7 36.1 %copy-start.7 = (f32[3072]{0:T(1024)S(1)}, f32[3072]{0:T(1024)}, u32[]{:S(2)}) copy-start(f32[3072]{0:T(1024)} %param.43) | copy-start | bytes 36868
  156.5 1.7 copy-start
  158.2 561.9 %all-gather.17.cloned.1.call-start = ((), (), s32[]{:S(2)}) async-start(), calls=%async_computation.5 | async-start | bytes 5898240 | tf_op jit(solution)/shard_map/all_gather | solution.py:594
  158.3 304.9 %collective-permute-start.5 = (bf16[1536,3072]{1,0:T(8,128)(2,1)}, bf16[1536,3072]{1,0:T(8,128)(2,1)}, u32[]{:S(2)}, u32[]{:S(2)}) collective-permute-start(bf16[1536,3072]{1,0:T(8,128)(2,1)} %get-tuple-element.41.y_ref.y0_ref), channel_id=1, source_target_pairs={{0,2},{1,3},{2,0},{3,1},{4,6},{5,7},{6,4},{7,5},{8,10},{9,11},{10,... | collective-permute-start | bytes 28311560 | tf_op jit(solution)/shard_map/ppermute | solution.py:589
  159.8 231.2 %collective-permute-start.3 = (f32[3072]{0:T(1024)S(1)}, f32[3072]{0:T(1024)S(1)}, u32[]{:S(2)}, u32[]{:S(2)}) collective-permute-start(f32[3072]{0:T(1024)S(1)} %copy-done.7), channel_id=1, source_target_pairs={{0,2},{1,3},{2,0},{3,1},{4,6},{5,7},{6,4},{7,5},{8,10},{9,11},{10,... | collective-permute-start | bytes 36872 | tf_op jit(solution)/shard_map/ppermute | solution.py:589
  161.7 228.2 %collective-permute-start.10 = (bf16[192,3072]{1,0:T(8,128)(2,1)S(1)}, bf16[192,3072]{1,0:T(8,128)(2,1)S(1)}, u32[]{:S(2)}, u32[]{:S(2)}) collective-permute-start(bf16[192,3072]{1,0:T(8,128)(2,1)S(1)} %constant_dynamic-slice_fusion), channel_id=1, source_target_pairs={{0,2},{1,3},{2,0},{3,1},{4,6},{5,7},{6,4},{7,5},{8,10},{9,11},{10,... | collective-permute-start | bytes 3538952 | tf_op jit(solution)/shard_map/ppermute | solution.py:589
  168.9 327.4 %collective-permute-start.4 = (bf16[256,3072]{1,0:T(8,128)(2,1)}, bf16[256,3072]{1,0:T(8,128)(2,1)}, u32[]{:S(2)}, u32[]{:S(2)}) collective-permute-start(bf16[256,3072]{1,0:T(8,128)(2,1)} %get-tuple-element.79), channel_id=1, source_target_pairs={{0,2},{1,3},{2,0},{3,1},{4,6},{5,7},{6,4},{7,5},{8,10},{9,11},{10,... | collective-permute-start | bytes 4718600 | tf_op jit(solution)/shard_map/ppermute | solution.py:589
  390.9 329.2 %all-gather.11.cloned.1.call-start = ((), (), s32[]{:S(2)}) async-start(), calls=%async_computation.2 | async-start | bytes 7864320 | tf_op jit(solution)/shard_map/all_gather | solution.py:594
  463.2 34.6 %collective-permute-start.7 = (bf16[1536,3072]{1,0:T(8,128)(2,1)}, bf16[1536,3072]{1,0:T(8,128)(2,1)}, u32[]{:S(2)}, u32[]{:S(2)}) collective-permute-start(bf16[1536,3072]{1,0:T(8,128)(2,1)} %collective-permute-done.5.y_ref), channel_id=1, source_target_pairs={{0,1},{1,0},{2,3},{3,2},{4,5},{5,4},{6,7},{7,6},{8,9},{9,8},{10,11... | collective-permute-start | bytes 28311560 | tf_op jit(solution)/shard_map/ppermute | solution.py:592
  463.3 33.1 %copy-start.2 = (bf16[256,3072]{1,0:T(8,128)(2,1)S(1)}, bf16[256,3072]{1,0:T(8,128)(2,1)}, u32[]{:S(2)}) copy-start(bf16[256,3072]{1,0:T(8,128)(2,1)} %get-tuple-element.78) | copy-start | bytes 4718596
  496.3 223.8 %all-gather.13.cloned.1.call-start = ((), (), s32[]{:S(2)}) async-start(), calls=%async_computation.3 | async-start | bytes 7864320 | tf_op jit(solution)/shard_map/all_gather | solution.py:594
  496.4 36.9 %collective-permute-start.6 = (bf16[256,3072]{1,0:T(8,128)(2,1)S(1)}, bf16[256,3072]{1,0:T(8,128)(2,1)}, u32[]{:S(2)}, u32[]{:S(2)}) collective-permute-start(bf16[256,3072]{1,0:T(8,128)(2,1)S(1)} %copy-done.2), channel_id=1, source_target_pairs={{0,2},{1,3},{2,0},{3,1},{4,6},{5,7},{6,4},{7,5},{8,10},{9,11},{10,... | collective-permute-start | bytes 4718600 | tf_op jit(solution)/shard_map/ppermute | solution.py:589
  497.9 35.5 %copy-start.1 = (bf16[256,3072]{1,0:T(8,128)(2,1)S(1)}, bf16[256,3072]{1,0:T(8,128)(2,1)}, u32[]{:S(2)}) copy-start(bf16[256,3072]{1,0:T(8,128)(2,1)} %get-tuple-element.77) | copy-start | bytes 4718596
  533.3 186.9 %all-gather.15.cloned.1.call-start = ((), (), s32[]{:S(2)}) async-start(), calls=%async_computation.4 | async-start | bytes 7864320 | tf_op jit(solution)/shard_map/all_gather | solution.py:594
  533.4 58.6 %collective-permute-start.8 = (bf16[256,3072]{1,0:T(8,128)(2,1)S(1)}, bf16[256,3072]{1,0:T(8,128)(2,1)S(1)}, u32[]{:S(2)}, u32[]{:S(2)}) collective-permute-start(bf16[256,3072]{1,0:T(8,128)(2,1)S(1)} %copy-done.1), channel_id=1, source_target_pairs={{0,2},{1,3},{2,0},{3,1},{4,6},{5,7},{6,4},{7,5},{8,10},{9,11},{10,... | collective-permute-start | bytes 4718600 | tf_op jit(solution)/shard_map/ppermute | solution.py:589
  591.9 128.2 %collective-permute-start.9 = (bf16[1536,768]{1,0:T(8,128)(2,1)}, bf16[1536,768]{1,0:T(8,128)(2,1)}, u32[]{:S(2)}, u32[]{:S(2)}) collective-permute-start(bf16[1536,768]{1,0:T(8,128)(2,1)} %attend.4), channel_id=1, source_target_pairs={{0,2},{1,3},{2,0},{3,1},{4,6},{5,7},{6,4},{7,5},{8,10},{9,11},{10,... | collective-permute-start | bytes 7077896 | tf_op jit(solution)/shard_map/ppermute | solution.py:589
  720.1 53.1 %copy-start.6 = (bf16[1536,768]{1,0:T(8,128)(2,1)S(1)}, bf16[1536,768]{1,0:T(8,128)(2,1)}, u32[]{:S(2)}) copy-start(bf16[1536,768]{1,0:T(8,128)(2,1)} %attend.5) | copy-start | bytes 7077892
  773.1 59.2 %collective-permute-start.12 = (f32[1536,3072]{1,0:T(8,128)}, f32[1536,3072]{1,0:T(8,128)}, u32[]{:S(2)}, u32[]{:S(2)}) collective-permute-start(f32[1536,3072]{1,0:T(8,128)} %out_rows.2), channel_id=1, source_target_pairs={{0,1},{1,0},{2,3},{3,2},{4,5},{5,4},{6,7},{7,6},{8,9},{9,8},{10,11... | collective-permute-start | bytes 56623112 | tf_op jit(solution)/shard_map/ppermute | solution.py:592
  773.2 59.1 %collective-permute-start.11 = (bf16[1536,768]{1,0:T(8,128)(2,1)S(1)}, bf16[1536,768]{1,0:T(8,128)(2,1)}, u32[]{:S(2)}, u32[]{:S(2)}) collective-permute-start(bf16[1536,768]{1,0:T(8,128)(2,1)S(1)} %copy-done.6), channel_id=1, source_target_pairs={{0,2},{1,3},{2,0},{3,1},{4,6},{5,7},{6,4},{7,5},{8,10},{9,11},{10,... | collective-permute-start | bytes 7077896 | tf_op jit(solution)/shard_map/ppermute | solution.py:589
  (4 other events, 4.0 us)
Sparse Core Ops, SparseCore 0:
  82.4 67.6 all-gather.6
  158.4 119.6 all-gather.8
  391.0 54.2 all-gather.16
  496.5 67.3 all-gather.10
  565.5 66.2 all-gather.12
  633.5 66.2 all-gather.14

commit v3 on v2

--- a/solution.py
+++ b/solution.py
@@ -27,7 +27,7 @@
 C_PAIRS = [(0, 1), (1, 0), (2, 3), (3, 2)]
 
 
-def params(mib=60, **kw):
+def params(mib=63, **kw):
     return pltpu.CompilerParams(vmem_limit_bytes=mib * 2 ** 20, **kw)
 
 
@@ -128,14 +128,15 @@
             grid_hw.reshape(2), cond, w_mod, b_mod[None], x, FREQ, qg, kg)
 
 
-QBM = 512
+QBM = 768
 SUB = 256
+SROW = 384
 
 
 def qkv_kernel(which_ref, sc_ref, y_ref, w_ref, b_ref, qg_ref, kg_ref, cos_ref, sin_ref, lim_in, _q, _k, _v,
                q_ref, k_ref, vt_ref, lim_ref, left0, left1):
     n = pl.program_id(1)
-    tiles = [(i, s) for i in range(QBM // SUB) for s in range(DQ // SUB)]
+    tiles = [(i, s) for i in range(QBM // SROW) for s in range(DQ // SUB)]
     pairs = [tiles[a:a + 2] for a in range(0, len(tiles), 2)]
 
     @pl.when(jnp.logical_and(pl.program_id(0) == 0, n == 0))
@@ -143,11 +144,11 @@
         lim_ref[...] = lim_in[...]
 
     def proj(t):
-        return jnp.dot(y_ref[pl.ds(t[0] * SUB, SUB), :], w_ref[0, :, pl.ds(t[1] * SUB, SUB)], preferred_element_type=F32)
+        return jnp.dot(y_ref[pl.ds(t[0] * SROW, SROW), :], w_ref[0, :, pl.ds(t[1] * SUB, SUB)], preferred_element_type=F32)
 
     def rope(r, t, gain, row, out_ref):
-        at = pl.ds(t[0] * SUB, SUB)
-        even = lax.broadcasted_iota(jnp.int32, (SUB, HD), 1) % 2 == 0
+        at = pl.ds(t[0] * SROW, SROW)
+        even = lax.broadcasted_iota(jnp.int32, (SROW, HD), 1) % 2 == 0
         for h in range(SUB // HD):
             lo = t[1] * SUB + h * HD
             x = r[:, h * HD:(h + 1) * HD] + b_ref[row:row + 1, lo:lo + HD]
@@ -159,8 +160,8 @@
     def put(r, t):
         lo = t[1] * SUB
         v = r + b_ref[2:3, lo:lo + SUB]
-        vt_ref[pl.ds(lo, SUB), pl.ds(t[0] * SUB, SUB)] = v.T.astype(BF)
-        top = jnp.max(jnp.abs(v).reshape(SUB // 8, 8, SUB), axis=0)
+        vt_ref[pl.ds(lo, SUB), pl.ds(t[0] * SROW, SROW)] = v.T.astype(BF)
+        top = jnp.max(jnp.abs(v).reshape(SROW // 8, 8, SUB), axis=0)
         lim_ref[...] = jnp.maximum(lim_ref[...], jnp.maximum(top[:, :HD], top[:, HD:]))
 
     def q_epi(r, t):
@@ -218,7 +219,7 @@
                        pl.BlockSpec((QBM, DQ), lambda i, n, w, s: (at(i, w, s), 0)),
                        pl.BlockSpec((DQ, QBM), lambda i, n, w, s: (0, at(i, w, s))),
                        full(8, HD)],
-            scratch_shapes=[pltpu.VMEM((SUB, SUB), F32)] * 2),
+            scratch_shapes=[pltpu.VMEM((SROW, SUB), F32)] * 2),
         out_shape=[jax.ShapeDtypeStruct((SEQ, DQ), BF), jax.ShapeDtypeStruct((SEQ, DQ), BF),
                    jax.ShapeDtypeStruct((DQ, SEQ), BF), jax.ShapeDtypeStruct((8, HD), F32)],
         input_output_aliases={10: 0, 11: 1, 12: 2}, compiler_params=params(),
@@ -256,14 +257,15 @@
 
         @pl.when(has_pad)
         def _():
-            s = lax.dot_general(k_ref[pl.ds(VID, TXT), :], q_ref[...], NT, preferred_element_type=F32)
+            last_q = pl.ds(bq - TXT, TXT)
+            s = lax.dot_general(k_ref[pl.ds(VID, TXT), :], q_ref[last_q, :], NT, preferred_element_type=F32)
             pad_key = lax.broadcasted_iota(jnp.int32, (TXT, 1), 0) >= txt_len
             s = jnp.where(pad_key, s, -1e30)
             p = jnp.exp2(s - jnp.max(s, axis=0, keepdims=True))
             lp = jnp.sum(p, axis=0, keepdims=True)
             ap = jnp.dot(vt_ref[:, pl.ds(VID, TXT)], p.astype(BF), preferred_element_type=F32)
-            row = first_row + lax.broadcasted_iota(jnp.int32, (bq, 1), 0)
-            o_ref[...] = jnp.where(row < VID + txt_len, o_ref[...].astype(F32), (ap * (1.0 / lp)).T).astype(BF)
+            row = lax.broadcasted_iota(jnp.int32, (TXT, 1), 0)
+            o_ref[last_q, :] = jnp.where(row < txt_len, o_ref[last_q, :].astype(F32), (ap * (1.0 / lp)).T).astype(BF)
 
     @pl.when(flag_ref[0] == 1)
     def _():
@@ -326,6 +328,7 @@
 NK = D // KC
 NX = D // HD
 NJ = D // BN
+NP = 3
 TILES = tuple((r, 256) for r in range(0, SHARD, 256))
 
 
@@ -359,7 +362,13 @@
         c.wait()
 
 
-def mlp_kernel(fused, y0_ref, y1_ref, wa_ref, wb_ref, b_ref, o_ref, xs, ws, sx, sw, sf, *more):
+def mlp_kernel(fused, *refs):
+    if fused:
+        sc_ref, y0_ref, y1_ref, wa_ref, wb_ref, b_ref, o_ref, *cut_refs = refs[:7 + NP]
+    else:
+        y0_ref, y1_ref, wa_ref, wb_ref, b_ref, o_ref = refs[:6]
+        cut_refs = []
+    xs, ws, sx, sw, sf, *more = refs[6 + len(cut_refs) + (1 if fused else 0):]
     i = pl.program_id(0)
     s = pl.program_id(1)
     steps = 2 * NJ if fused else NJ
@@ -408,6 +417,27 @@
     def _():
         for c in range(NK):
             waited(copy_x(y1_ref, 1, c))
+
+    if fused:
+        qs, sq_in, sq_out = more[1:]
+        t = i * steps + s
+        size = D // NP // 4
+        rows = lambda p: pl.ds(pl.multiple_of(p * (D // NP) + sc_ref[5] * size, size), size)
+        cut_in = lambda: [pltpu.make_async_copy(wb_ref.at[rows(p), :], qs.at[p], sq_in.at[p]) for p in range(NP)]
+        cut_out = lambda: [pltpu.make_async_copy(qs.at[p], cut_refs[p], sq_out.at[p]) for p in range(NP)]
+
+        @pl.when(t == 2)
+        def _():
+            started(cut_in())
+
+        @pl.when(t == 5)
+        def _():
+            waited(cut_in())
+            started(cut_out())
+
+        @pl.when(t == 9)
+        def _():
+            waited(cut_out())
 
     bias = b_ref[:, pl.ds(pl.multiple_of(jnp.minimum(s, NJ - 1) * BN, BN), BN)]
 
@@ -452,7 +482,7 @@
             tiled(lambda tile: dot([more[0][x, pl.ds(*tile), :] for x in range(NX)], weights()), store)
 
 
-def mlp(fused, y0, y1, wa, wb, b):
+def mlp(fused, y0, y1, wa, wb, b, sc=None):
     steps = 2 * NJ if fused else NJ
     anyspec = pl.BlockSpec(memory_space=pl.ANY)
     dma = pltpu.SemaphoreType.DMA
@@ -460,17 +490,25 @@
         omap = lambda i, s: (jnp.where(s >= NJ, i, 0), jnp.where(s >= NJ, s - NJ, jnp.where(i == 0, 0, NJ - 1)))
     else:
         omap = lambda i, s: (i, s)
+    in_specs = [anyspec] * 4 + [pl.BlockSpec((1, D), lambda i, s: (0, 0))]
+    out_specs = [pl.BlockSpec((SHARD, BN), omap)]
+    out_shape = [jax.ShapeDtypeStruct((CHIP, D), F32 if fused else BF)]
     scratch = [pltpu.VMEM((2, NX, SHARD, HD), BF), pltpu.VMEM((2, NL, D, HD), BF), dma((2, NX)), dma((2, NL)), dma((NK, NL))]
+    args = [y0, y1, wa, wb, b]
+    if fused:
+        size = D // NP // 4
+        in_specs.insert(0, pl.BlockSpec(memory_space=pltpu.SMEM))
+        args.insert(0, sc)
+        out_specs += [anyspec] * NP
+        out_shape += [jax.ShapeDtypeStruct((size, D), BF)] * NP
+        scratch += [pltpu.VMEM((NX, SHARD, HD), BF), pltpu.VMEM((NP, size, D), BF), dma((NP,)), dma((NP,))]
     return pl.pallas_call(
-        functools.partial(mlp_kernel, fused), grid=(2, steps),
-        in_specs=[anyspec] * 4 + [pl.BlockSpec((1, D), lambda i, s: (0, 0))],
-        out_specs=pl.BlockSpec((SHARD, BN), omap), out_shape=jax.ShapeDtypeStruct((CHIP, D), F32 if fused else BF),
-        scratch_shapes=scratch + ([pltpu.VMEM((NX, SHARD, HD), BF)] if fused else []),
-        compiler_params=params(), cost_estimate=cost(2 * CHIP * D * steps * BN, CHIP * D * 8), name="mlp")(y0, y1, wa, wb, b)
+        functools.partial(mlp_kernel, fused), grid=(2, steps), in_specs=in_specs, out_specs=out_specs, out_shape=out_shape,
+        scratch_shapes=scratch, compiler_params=params(63),
+        cost_estimate=cost(2 * CHIP * D * steps * BN, CHIP * D * 8), name="mlp")(*args)
 
 
 KO = D + 2 * DQ
-NP = 3
 OCHUNKS = tuple((c * KC, KC) for c in range(NK)) + ((D, DQ), (D + DQ, DQ))
 
 
@@ -597,14 +635,12 @@
         split = D // 3
         hop_in = [swap_x(lax.dynamic_slice(w_mlp_in, (dp * q4, lo), (q4, n)))
                   for lo, n in ((0, split), (split, D - split))]
-        hop_att = swap_x(lax.dynamic_slice_in_dim(w_out_attn, dp * (DQ // 4), DQ // 4, 0))
-        hop_out = [swap_x(lax.dynamic_slice_in_dim(w_out_mlp, c * split + dp * (split // 4), split // 4, 0)) for c in range(NP)]
         b_in_o = swap_x(b_mlp_in)[None]
 
         sib = tp + 1 - 2 * own
         rem = (tp + 2) % 4
         remsib = (sib + 2) % 4
-        sc = jnp.stack([tp, sib, rem, remsib, txt_len[0]]).astype(jnp.int32)
+        sc = jnp.stack([tp, sib, rem, remsib, txt_len[0], dp]).astype(jnp.int32)
         OWN, SIB, REM, REMSIB = (np.full((1,), i, np.int32) for i in range(4))
 
         qg = q_gain[None]
@@ -618,9 +654,10 @@
         *bufs, lim = qkv(OWN, sc, y, *tabs, lim, bufs)
         *bufs, lim = qkv(SIB, sc, y_sib, *tabs, lim, bufs)
         w_in_o1 = gather(after(hop_in[1], lim))
-        part = mlp(True, y, after(y_sib, lim), w_mlp_in, w_out_mlp, b_mlp_in[None])
-        w_att_o = gather(after(hop_att, part))
-        m_oth = mlp(False, y, y_sib, w_in_o0, w_in_o1, b_in_o)
+        part, *cut = mlp(True, y, after(y_sib, lim), w_mlp_in, w_out_mlp, b_mlp_in[None], sc)
+        hop_out = [swap_x(c) for c in cut]
+        w_att_o = swap_x(w_out_attn)
+        m_oth, = mlp(False, y, y_sib, w_in_o0, w_in_o1, b_in_o)
         y_rem = after(y_rem, m_oth)
         y_remsib = swap_c(y_rem)
         *bufs, lim = qkv(REM, sc, y_rem, *tabs, lim, bufs)

time: 902 us -> 944 us (1.047)
  waiting for transfers between devices: 146 us -> 214 us
  local copies, waits for them, and re-layouts: 21 us -> 10 us
    ppermute x10, waiting for transfers between devices: 146 us -> 214 us  [swap_x(): return lax.ppermute(v, 'tp', X_PAIRS)]
  transfers between devices with their start and end apart: 19 -> 18, of which waited for: 4 -> 6; matrix products, arithmetic and copies ran while one was open for 2% -> 1% of each run, Pallas kernels for 62% -> 58%
where the time goes in v3:
time: 944 us; the launch traced here: 941 us
  Pallas kernels  685 us (73%)
  waiting for transfers between devices  214 us (23%)
  starting transfers between devices  17.3 us (2%)
  between operations  14.4 us (2%)
  local copies, waits for them, and re-layouts  10 us (1%)
    ppermute x10, waiting for transfers between devices, swap_x(): return lax.ppermute(v, 'tp', X_PAIRS)  214 us
    pallas_call x2, Pallas kernels, mlp(): pl.pallas_call(functools.partial(mlp_kernel, fused), grid=(2, steps), in_...  207 us
    pallas_call x4, Pallas kernels, attend(): pl.pallas_call(attn_kernel, grid_spec=pltpu.PrefetchScalarGridSpec(num_sc...  207 us
    pallas_call x4, Pallas kernels, qkv(): pl.pallas_call(qkv_kernel, grid_spec=pltpu.PrefetchScalarGridSpec(num_sca...  129 us
    pallas_call x2, Pallas kernels, out_rows(): pl.pallas_call(functools.partial(out_kernel, final, first_row, a0_row), g...  107 us
    pallas_call x1, Pallas kernels, prep(): pl.pallas_call(prep_kernel, grid_spec=pltpu.PrefetchScalarGridSpec(num_sc...  34.7 us
  transfers between devices with their start and end apart: 18, of which 6 were waited for; matrix products, arithmetic and copies ran while one was open for 1% of the time, Pallas kernels for 58%

profile of v3, /device:TPU:0, one launch (start us, length us, event | category | flops | bytes accessed | tf_op | source)
XLA Modules:
  0.0 940.8 jit_solution(11864976557558612358)
XLA Ops:
  6.5 34.7 %prep.1 = (bf16[1536,3072]{1,0:T(8,128)(2,1)}, f32[6144,128]{1,0:T(8,128)}, f32[6144,128]{1,0:T(8,128)}, f32[1,3072]{1,0:T(1,128)}, f32[8,128]{1,0:T(8,128)}, /*...) custom-call(s32[2]{0:T(128)} %bitcast.25, f32[1,3072]{1,0:T(1,128)} %c_ref.1, ...), custom_call_target="tpu_custom_call" | custom-call | flops 20000000000 | bytes 90000000 | tf_op jit(solution)/shard_map/prep/pallas_call | solution.py:114
  43.5 2.5 collective-permute-start.1
  46.0 35.0 %collective-permute-done.1 = bf16[768,1024]{1,0:T(8,128)(2,1)S(1)} collective-permute-done((bf16[768,1024]{1,0:T(8,128)(2,1)S(1)}, bf16[768,1024]{1,0:T(8,128)(2,1)S(1)}, u32[]{:S(2)}, u32[]{:S(2)}) %collective-permute-start.1) | collective-permute-done | bytes 1572896 | tf_op jit(solution)/shard_map/ppermute | solution.py:627
  82.5 3.9 constant_dynamic-slice_fusion
  86.5 1.7 collective-permute-start.2
  89.6 32.2 %qkv.4 = (bf16[6144,768]{1,0:T(8,128)(2,1)}, bf16[6144,768]{1,0:T(8,128)(2,1)}, bf16[768,6144]{1,0:T(8,128)(2,1)}, f32[8,128]{1,0:T(8,128)}) custom-call(s32[1]{0:T(128)} %constant.71.clone.which_ref, s32[6]{0:T(128)} %stack.23.sc_ref.refs_0_, ...), custom_call_target="tpu_custom_call", output_to_operand_aliasing={{0}: (10, {}), {1}: (11, {}), {2}: (12, {})} | custom-call | flops 21743271936 | bytes 23592960 | tf_op jit(solution)/shard_map/qkv/pallas_call | solution.py:208
  121.8 31.9 %qkv.5 = (bf16[6144,768]{1,0:T(8,128)(2,1)}, bf16[6144,768]{1,0:T(8,128)(2,1)}, bf16[768,6144]{1,0:T(8,128)(2,1)}, f32[8,128]{1,0:T(8,128)}) custom-call(s32[1]{0:T(128)} %constant.72.clone.which_ref, s32[6]{0:T(128)} %stack.23.sc_ref.refs_0_, ...), custom_call_target="tpu_custom_call", output_to_operand_aliasing={{0}: (10, {}), {1}: (11, {}), {2}: (12, {})} | custom-call | flops 21743271936 | bytes 23592960 | tf_op jit(solution)/shard_map/qkv/pallas_call | solution.py:208
  153.6 3.1 collective-permute-done.2
  158.8 135.7 %mlp.3 = (f32[3072,3072]{1,0:T(8,128)}, bf16[256,3072]{1,0:T(8,128)(2,1)}, bf16[256,3072]{1,0:T(8,128)(2,1)}, bf16[256,3072]{1,0:T(8,128)(2,1)}) custom-call(s32[6]{0:T(128)} %stack.23.sc_ref.refs_0_, bf16[1536,3072]{1,0:T(8,128)(2,1)} %get-tuple-element.44.y_ref.refs_0_.refs_1_, bf16[1536,3072]{1,0:T(8,128)(2,1)} %collective-permute-done.y_ref.refs_1_.refs_2_, ...), custom_call_target="tpu_custom_call" | custom-call | flops 115964116992 | bytes 75497472 | tf_op jit(solution)/shard_map/mlp/pallas_call | solution.py:505
  296.0 67.1 %collective-permute-done.3 = f32[3072]{0:T(1024)S(1)} collective-permute-done((f32[3072]{0:T(1024)S(1)}, f32[3072]{0:T(1024)S(1)}, u32[]{:S(2)}, u32[]{:S(2)}) %collective-permute-start.3) | collective-permute-done | bytes 12320 | tf_op jit(solution)/shard_map/ppermute | solution.py:627
  363.7 71.6 %mlp.2.refs_0_ = bf16[3072,3072]{1,0:T(8,128)(2,1)} custom-call(bf16[1536,3072]{1,0:T(8,128)(2,1)} %get-tuple-element.44.y_ref.refs_0_.refs_1_, bf16[1536,3072]{1,0:T(8,128)(2,1)} %collective-permute-done.y_ref.refs_1_.refs_2_, bf16[3072,1024]{1,0:T(8,128)(2,1)} %all-gather.6.cloned.1.call-done.refs_2_, ...), custom_call_target="tpu_custom_call" | custom-call | flops 57982058496 | bytes 75497472 | tf_op jit(solution)/shard_map/mlp/pallas_call | solution.py:505
  435.4 31.8 %qkv.6 = (bf16[6144,768]{1,0:T(8,128)(2,1)}, bf16[6144,768]{1,0:T(8,128)(2,1)}, bf16[768,6144]{1,0:T(8,128)(2,1)}, f32[8,128]{1,0:T(8,128)}) custom-call(s32[1]{0:T(128)} %constant.73.clone.which_ref, s32[6]{0:T(128)} %stack.23.sc_ref.refs_0_, ...), custom_call_target="tpu_custom_call", output_to_operand_aliasing={{0}: (10, {}), {1}: (11, {}), {2}: (12, {})} | custom-call | flops 21743271936 | bytes 23592960 | tf_op jit(solution)/shard_map/qkv/pallas_call | solution.py:208
  467.3 1.6 collective-permute-start.6
  468.9 33.1 %qkv.7 = (bf16[6144,768]{1,0:T(8,128)(2,1)}, bf16[6144,768]{1,0:T(8,128)(2,1)}, bf16[768,6144]{1,0:T(8,128)(2,1)}, f32[8,128]{1,0:T(8,128)}) custom-call(s32[1]{0:T(128)} %constant.74.clone.which_ref, s32[6]{0:T(128)} %stack.23.sc_ref.refs_0_, ...), custom_call_target="tpu_custom_call", output_to_operand_aliasing={{0}: (10, {}), {1}: (11, {}), {2}: (12, {})} | custom-call | flops 21743271936 | bytes 23592960 | tf_op jit(solution)/shard_map/qkv/pallas_call | solution.py:208
  501.9 2.5 collective-permute-done.6
  507.6 54.0 %attend.4 = bf16[1536,768]{1,0:T(8,128)(2,1)} custom-call(s32[16]{0:T(128)} %constant.75.clone.head_ref, s32[16]{0:T(128)} %call_exported.0.which_ref, s32[16]{0:T(128)} %call_exported.1.row_ref.which_ref, s32[6]{0:T(128)} %stack.23.sc_ref.refs_0_, f32[8,128]{1,0:T(8,128)} %get-tuple-element.70.lim_ref, bf16[6144,768]{1,0:T(8,128)(2,1)} %get-tuple-element.73.q_ref, ...), custom_call_target="tpu_custom_call" | custom-call | flops 43486543872 | bytes 23592960 | tf_op jit(solution)/shard_map/attend/pallas_call | solution.py:315
  561.6 81.6 %collective-permute-done.8 = bf16[256,3072]{1,0:T(8,128)(2,1)} collective-permute-done((bf16[256,3072]{1,0:T(8,128)(2,1)}, bf16[256,3072]{1,0:T(8,128)(2,1)}, u32[]{:S(2)}, u32[]{:S(2)}) %collective-permute-start.8) | collective-permute-done | bytes 1572896 | tf_op jit(solution)/shard_map/ppermute | solution.py:627
  643.8 51.0 %attend.5 = bf16[1536,768]{1,0:T(8,128)(2,1)} custom-call(s32[16]{0:T(128)} %constant.75.clone.head_ref, s32[16]{0:T(128)} %call_exported.2.which_ref, s32[16]{0:T(128)} %call_exported.1.row_ref.which_ref, s32[6]{0:T(128)} %stack.23.sc_ref.refs_0_, f32[8,128]{1,0:T(8,128)} %get-tuple-element.70.lim_ref, bf16[6144,768]{1,0:T(8,128)(2,1)} %get-tuple-element.73.q_ref, ...), custom_call_target="tpu_custom_call" | custom-call | flops 43486543872 | bytes 23592960 | tf_op jit(solution)/shard_map/attend/pallas_call | solution.py:315
  694.8 74.6 %attend.6.refs_4_.refs_0_ = bf16[3072,768]{1,0:T(8,128)(2,1)} custom-call(s32[16]{0:T(128)} %constant.79.clone.head_ref, s32[16]{0:T(128)} %constant.80.clone.which_ref, s32[16]{0:T(128)} %constant.81.clone.row_ref, s32[6]{0:T(128)} %stack.23.sc_ref.refs_0_, f32[8,128]{1,0:T(8,128)} %get-tuple-element.70.lim_ref, bf16[6144,768]{1,0:T(8,128)(2,1)} %get-tuple-element.73.q_ref, ...), custom_call_target="tpu_custom_call" | custom-call | flops 65229815808 | bytes 35389440 | tf_op jit(solution)/shard_map/attend/pallas_call | solution.py:315
  769.5 52.5 %out_rows.2 = f32[1536,3072]{1,0:T(8,128)} custom-call(bf16[3072,3072]{1,0:T(8,128)(2,1)} %mlp.2.refs_0_, bf16[1024,3072]{1,0:T(8,128)(2,1)} %all-gather.10.cloned.1.call-done.refs_1_, bf16[1024,3072]{1,0:T(8,128)(2,1)} %all-gather.12.cloned.1.call-done.refs_2_, bf16[1024,3072]{1,0:T(8,128)(2,1)} %all-gather.14.cloned.1.call-done.refs_3_, ...), custom_call_target="tpu_custom_call" | custom-call | flops 43486543872 | bytes 66060288 | tf_op jit(solution)/shard_map/out_rows/pallas_call | solution.py:606
  822.6 4.1 collective-permute-start.11
  827.3 27.2 %attend.7.refs_4_ = bf16[3072,768]{1,0:T(8,128)(2,1)} custom-call(s32[16]{0:T(128)} %constant.82.clone.head_ref, s32[16]{0:T(128)} %call_exported.1.row_ref.which_ref, s32[16]{0:T(128)} %call_exported.3.row_ref, s32[6]{0:T(128)} %stack.23.sc_ref.refs_0_, f32[8,128]{1,0:T(8,128)} %get-tuple-element.70.lim_ref, ...), custom_call_target="tpu_custom_call", output_to_operand_aliasing={{}: (8, {})} | custom-call | flops 21743271936 | bytes 11796480 | tf_op jit(solution)/shard_map/attend/pallas_call | solution.py:315
  854.5 24.4 %collective-permute-done.11.refs_5_ = bf16[1536,768]{1,0:T(8,128)(2,1)} collective-permute-done((bf16[1536,768]{1,0:T(8,128)(2,1)}, bf16[1536,768]{1,0:T(8,128)(2,1)}, u32[]{:S(2)}, u32[]{:S(2)}) %collective-permute-start.11) | collective-permute-done | bytes 2359328 | tf_op jit(solution)/shard_map/ppermute | solution.py:627
  878.9 54.9 %out_rows.3 = bf16[1536,3072]{1,0:T(8,128)(2,1)} custom-call(bf16[3072,3072]{1,0:T(8,128)(2,1)} %mlp.2.refs_0_, bf16[1024,3072]{1,0:T(8,128)(2,1)} %all-gather.10.cloned.1.call-done.refs_1_, bf16[1024,3072]{1,0:T(8,128)(2,1)} %all-gather.12.cloned.1.call-done.refs_2_, bf16[1024,3072]{1,0:T(8,128)(2,1)} %all-gather.14.cloned.1.call-done.refs_3_, ...), custom_call_target="tpu_custom_call" | custom-call | flops 43486543872 | bytes 66060288 | tf_op jit(solution)/shard_map/out_rows/pallas_call | solution.py:606
  (43 shorter events, 13.6 us)
Async XLA Ops:
  6.5 356.6 %all-gather.6.cloned.1.call-start = ((), (), s32[]{:S(2)}) async-start(), calls=%async_computation | async-start | bytes 7864320 | tf_op jit(solution)/shard_map/all_gather | solution.py:632
  41.2 80.5 %collective-permute-start = (bf16[1536,3072]{1,0:T(8,128)(2,1)}, bf16[1536,3072]{1,0:T(8,128)(2,1)}, u32[]{:S(2)}, u32[]{:S(2)}) collective-permute-start(bf16[1536,3072]{1,0:T(8,128)(2,1)} %get-tuple-element.44.y_ref.refs_0_.refs_1_), channel_id=1, source_target_pairs={{0,1},{1,0},{2,3},{3,2},{4,5},{5,4},{6,7},{7,6},{8,9},{9,8},{10,11... | collective-permute-start | bytes 28311560 | tf_op jit(solution)/shard_map/ppermute | solution.py:630
  43.5 37.6 %collective-permute-start.1 = (bf16[768,1024]{1,0:T(8,128)(2,1)S(1)}, bf16[768,1024]{1,0:T(8,128)(2,1)S(1)}, u32[]{:S(2)}, u32[]{:S(2)}) collective-permute-start(bf16[768,1024]{1,0:T(8,128)(2,1)S(1)} %constant_dynamic-slice_fusion.1), channel_id=1, source_target_pairs={{0,2},{1,3},{2,0},{3,1},{4,6},{5,7},{6,4},{7,5},{8,10},{9,11},{10,... | collective-permute-start | bytes 4718600 | tf_op jit(solution)/shard_map/ppermute | solution.py:627
  81.1 1.2 copy-start
  82.3 280.8 %all-gather.8.cloned.1.call-start = ((), (), s32[]{:S(2)}) async-start(), calls=%async_computation.1 | async-start | bytes 15728640 | tf_op jit(solution)/shard_map/all_gather | solution.py:632
  86.5 70.2 %collective-permute-start.2 = (bf16[768,2048]{1,0:T(8,128)(2,1)}, bf16[768,2048]{1,0:T(8,128)(2,1)}, u32[]{:S(2)}, u32[]{:S(2)}) collective-permute-start(bf16[768,2048]{1,0:T(8,128)(2,1)} %constant_dynamic-slice_fusion), channel_id=1, source_target_pairs={{0,2},{1,3},{2,0},{3,1},{4,6},{5,7},{6,4},{7,5},{8,10},{9,11},{10,... | collective-permute-start | bytes 9437192 | tf_op jit(solution)/shard_map/ppermute | solution.py:627
  121.7 36.5 %copy-start.1 = (f32[3072]{0:T(1024)S(1)}, f32[3072]{0:T(1024)}, u32[]{:S(2)}) copy-start(f32[3072]{0:T(1024)} %param.43) | copy-start | bytes 36868
  156.7 612.8 %all-gather.10.cloned.1.call-start = ((), (), s32[]{:S(2)}) async-start(), calls=%async_computation.2 | async-start | bytes 7864320 | tf_op jit(solution)/shard_map/all_gather | solution.py:632
  156.8 278.6 %collective-permute-start.5 = (bf16[1536,3072]{1,0:T(8,128)(2,1)}, bf16[1536,3072]{1,0:T(8,128)(2,1)}, u32[]{:S(2)}, u32[]{:S(2)}) collective-permute-start(bf16[1536,3072]{1,0:T(8,128)(2,1)} %get-tuple-element.44.y_ref.refs_0_.refs_1_), channel_id=1, source_target_pairs={{0,2},{1,3},{2,0},{3,1},{4,6},{5,7},{6,4},{7,5},{8,10},{9,11},{10,... | collective-permute-start | bytes 28311560 | tf_op jit(solution)/shard_map/ppermute | solution.py:627
  158.3 204.8 %collective-permute-start.3 = (f32[3072]{0:T(1024)S(1)}, f32[3072]{0:T(1024)S(1)}, u32[]{:S(2)}, u32[]{:S(2)}) collective-permute-start(f32[3072]{0:T(1024)S(1)} %copy-done.1), channel_id=1, source_target_pairs={{0,2},{1,3},{2,0},{3,1},{4,6},{5,7},{6,4},{7,5},{8,10},{9,11},{10,... | collective-permute-start | bytes 36872 | tf_op jit(solution)/shard_map/ppermute | solution.py:627
  294.6 172.6 %collective-permute-start.4 = (bf16[256,3072]{1,0:T(8,128)(2,1)}, bf16[256,3072]{1,0:T(8,128)(2,1)}, u32[]{:S(2)}, u32[]{:S(2)}) collective-permute-start(bf16[256,3072]{1,0:T(8,128)(2,1)} %get-tuple-element.59), channel_id=1, source_target_pairs={{0,2},{1,3},{2,0},{3,1},{4,6},{5,7},{6,4},{7,5},{8,10},{9,11},{10,... | collective-permute-start | bytes 4718600 | tf_op jit(solution)/shard_map/ppermute | solution.py:627
  363.1 0.6 copy-start.2
  435.3 33.5 %collective-permute-start.7 = (bf16[1536,3072]{1,0:T(8,128)(2,1)}, bf16[1536,3072]{1,0:T(8,128)(2,1)}, u32[]{:S(2)}, u32[]{:S(2)}) collective-permute-start(bf16[1536,3072]{1,0:T(8,128)(2,1)} %collective-permute-done.5.y_ref), channel_id=1, source_target_pairs={{0,1},{1,0},{2,3},{3,2},{4,5},{5,4},{6,7},{7,6},{8,9},{9,8},{10,11... | collective-permute-start | bytes 28311560 | tf_op jit(solution)/shard_map/ppermute | solution.py:630
  467.2 302.3 %all-gather.12.cloned.1.call-start = ((), (), s32[]{:S(2)}) async-start(), calls=%async_computation.3 | async-start | bytes 7864320 | tf_op jit(solution)/shard_map/all_gather | solution.py:632
  467.3 37.2 %collective-permute-start.6 = (bf16[256,3072]{1,0:T(8,128)(2,1)}, bf16[256,3072]{1,0:T(8,128)(2,1)}, u32[]{:S(2)}, u32[]{:S(2)}) collective-permute-start(bf16[256,3072]{1,0:T(8,128)(2,1)} %get-tuple-element.66), channel_id=1, source_target_pairs={{0,2},{1,3},{2,0},{3,1},{4,6},{5,7},{6,4},{7,5},{8,10},{9,11},{10,... | collective-permute-start | bytes 4718600 | tf_op jit(solution)/shard_map/ppermute | solution.py:627
  504.4 265.1 %all-gather.14.cloned.1.call-start = ((), (), s32[]{:S(2)}) async-start(), calls=%async_computation.4 | async-start | bytes 7864320 | tf_op jit(solution)/shard_map/all_gather | solution.py:632
  504.5 265.0 %collective-permute-start.10 = (bf16[768,3072]{1,0:T(8,128)(2,1)}, bf16[768,3072]{1,0:T(8,128)(2,1)}, u32[]{:S(2)}, u32[]{:S(2)}) collective-permute-start(bf16[768,3072]{1,0:T(8,128)(2,1)} %refs_6_.3), channel_id=1, source_target_pairs={{0,2},{1,3},{2,0},{3,1},{4,6},{5,7},{6,4},{7,5},{8,10},{9,11},{10,... | collective-permute-start | bytes 14155784 | tf_op jit(solution)/shard_map/ppermute | solution.py:627
  506.1 137.2 %collective-permute-start.8 = (bf16[256,3072]{1,0:T(8,128)(2,1)}, bf16[256,3072]{1,0:T(8,128)(2,1)}, u32[]{:S(2)}, u32[]{:S(2)}) collective-permute-start(bf16[256,3072]{1,0:T(8,128)(2,1)} %get-tuple-element.72), channel_id=1, source_target_pairs={{0,2},{1,3},{2,0},{3,1},{4,6},{5,7},{6,4},{7,5},{8,10},{9,11},{10,... | collective-permute-start | bytes 4718600 | tf_op jit(solution)/shard_map/ppermute | solution.py:627
  561.6 207.9 %collective-permute-start.9 = (bf16[1536,768]{1,0:T(8,128)(2,1)}, bf16[1536,768]{1,0:T(8,128)(2,1)}, u32[]{:S(2)}, u32[]{:S(2)}) collective-permute-start(bf16[1536,768]{1,0:T(8,128)(2,1)} %attend.4), channel_id=1, source_target_pairs={{0,2},{1,3},{2,0},{3,1},{4,6},{5,7},{6,4},{7,5},{8,10},{9,11},{10,... | collective-permute-start | bytes 7077896 | tf_op jit(solution)/shard_map/ppermute | solution.py:627
  822.1 56.9 %collective-permute-start.12 = (f32[1536,3072]{1,0:T(8,128)}, f32[1536,3072]{1,0:T(8,128)}, u32[]{:S(2)}, u32[]{:S(2)}) collective-permute-start(f32[1536,3072]{1,0:T(8,128)} %out_rows.2), channel_id=1, source_target_pairs={{0,1},{1,0},{2,3},{3,2},{4,5},{5,4},{6,7},{7,6},{8,9},{9,8},{10,11... | collective-permute-start | bytes 56623112 | tf_op jit(solution)/shard_map/ppermute | solution.py:630
  822.6 56.3 %collective-permute-start.11 = (bf16[1536,768]{1,0:T(8,128)(2,1)}, bf16[1536,768]{1,0:T(8,128)(2,1)}, u32[]{:S(2)}, u32[]{:S(2)}) collective-permute-start(bf16[1536,768]{1,0:T(8,128)(2,1)} %attend.5), channel_id=1, source_target_pairs={{0,2},{1,3},{2,0},{3,1},{4,6},{5,7},{6,4},{7,5},{8,10},{9,11},{10,... | collective-permute-start | bytes 7077896 | tf_op jit(solution)/shard_map/ppermute | solution.py:627
Sparse Core Ops, SparseCore 0:
  82.4 67.6 all-gather.5
  156.9 119.6 all-gather.7
  467.3 67.5 all-gather.9
  536.6 66.2 all-gather.11
  643.4 67.4 all-gather.13
